TPU v7x, 32 devices: a whole 2x2x4 slice. The times are simulated.
32 devices in a mesh: row: 4 (over z), col: 8 (over y, x, core).
Axes of the slice: x: 2, y: 2, z: 4, core: 2. Of those that a mesh axis runs over, the one named last changes fastest.
Arguments:
- a_matrix: bfloat16 [8192, 8192], P('row', 'col'), may hold values from -6 to 6
- a_flags: int32 [64, 64], P('row', 'col'), may hold values from 0 to 1, as said below
- b_matrix: bfloat16 [8192, 16384], P('row', 'col'), may hold values from -0.1875 to 0.1875
- b_flags: int32 [64, 128], P('row', 'col'), may hold values from 0 to 1, as said below
- sections: int32 [2], replicated, may hold values from 0 to 7
Outputs:
- packed: bfloat16 [8192, 16384], P('row', 'col')
- tile_place: int32 [64, 128], P('row', 'col')
Inputs may be any that keep to these rules, and one draw needn't show every extreme that they name: `a_flags`: 0 or 1; the 16 x 8 tiles of one device hold at most 64 ones, and some device holds exactly 64. `b_flags`: 0 or 1; each aligned block of 8 x 16 tiles holds at most 64 ones, and some block exactly 64.
All inputs are finite; a program needn't handle non-finite values.
Results may differ from a plain program's by a relative error of at most 0.001.
Values may be sent and summed in bfloat16 or wider, within the bound.
A program may use at most 128 MiB of HBM per device.

v0:
```python
import functools

import jax
import jax.numpy as jnp
from jax import lax
from jax.experimental import pallas as pl
from jax.experimental.pallas import tpu as pltpu
from jax.sharding import PartitionSpec as P

TILE = 128
SECTIONS = 2
MOST = 64
CHUNKS = 16
MESH = pl.DeviceIdType.MESH
ANY = pl.BlockSpec(memory_space=pl.ANY)
SMEM = pl.BlockSpec(memory_space=pltpu.SMEM)
VMEM = pl.BlockSpec(memory_space=pltpu.VMEM)


def ring_place(index, n):
    half = n // 2
    turned = half + lax.rem(index - half + n // 4 + half, half)
    return jnp.where(index < half, index, turned)


def tile_at(ref, p, q):
    rows = pl.ds(pl.multiple_of(p * TILE, TILE), TILE)
    cols = pl.ds(q * TILE if isinstance(q, int) else pl.multiple_of(q * TILE, TILE), TILE)
    return ref.at[rows, cols]


def pack_kernel(tile_rows, panel, tile_cols, ratio, sections, a_flags, b_flags, a, b, a_out, b0_out, b1_out, sem):
    def gather(flags, src, out, rows, cols, first):
        def lap(p, rank):
            for q in range(cols):
                here = flags[first + p, q]

                @pl.when(here == 1)
                def _():
                    pltpu.make_async_copy(tile_at(src, first + p, q), out.at[rank], sem).start()

                rank = rank + here
            return rank

        return lax.fori_loop(0, rows, lap, jnp.int32(0))

    total = jnp.int32(0)
    my_row, my_col = lax.axis_index("row"), lax.axis_index("col")
    mine_a = (sections[0] == my_col) | (sections[1] == my_col)
    total += lax.cond(mine_a, lambda: gather(a_flags, a, a_out, tile_rows, panel, 0), lambda: jnp.int32(0))
    for s, out in ((0, b0_out), (1, b1_out)):
        first = lax.rem(sections[s], ratio) * panel
        total += lax.cond(
            sections[s] // ratio == my_row,
            lambda: gather(b_flags, b, out, panel, tile_cols, first),
            lambda: jnp.int32(0),
        )

    @pl.loop(0, total)
    def _(i):
        pltpu.make_async_copy(tile_at(a, 0, 0), a_out.at[0], sem).wait()


def spread_kernel(root, owner, n_row, n_col, with_flags, *refs):
    if with_flags:
        a_src, b_src, flags, a_dst, b_dst, every, *sems = refs
        a_next, a_prev, a_recv, b_up, b_down, b_recv, local, row_send, row_recv, col_send, col_recv = sems
    else:
        a_src, b_src, a_dst, b_dst, a_next, a_prev, a_recv, b_up, b_down, b_recv = refs
    my_row, my_col = lax.axis_index("row"), lax.axis_index("col")
    span = MOST // CHUNKS
    half = n_col // 2
    root_place = root if root < half else half + (root - half + n_col // 4) % half
    place = ring_place(my_col, n_col)
    dist = lax.rem(place - root_place + n_col, n_col)
    nxt = ring_place(lax.rem(place + 1, n_col), n_col)
    prv = ring_place(lax.rem(place + n_col - 1, n_col), n_col)
    a_root, b_root = dist == 0, my_row == owner
    to_next = dist < half
    to_prev = (dist == 0) | (dist > half + 1)
    to_up = (my_row >= owner) & (my_row < n_row - 1)
    to_down = (my_row <= owner) & (my_row > 0)
    up = jnp.minimum(my_row + 1, n_row - 1)
    down = jnp.maximum(my_row - 1, 0)

    barrier = pltpu.get_barrier_semaphore()

    def ready(when, row, col):
        @pl.when(when)
        def _():
            pl.semaphore_signal(barrier, inc=1, device_id=(row, col), device_id_type=MESH)

    if with_flags:
        for k in range(1, n_row):
            ready(True, lax.rem(my_row + k, n_row), my_col)
        for k in range(1, n_col):
            ready(True, my_row, lax.rem(my_col + k, n_col))
        pl.semaphore_wait(barrier, n_row + n_col - 2)
    else:
        ready((dist > 0) & (dist <= half), my_row, prv)
        ready(dist > half, my_row, nxt)
        ready(my_row > owner, down, my_col)
        ready(my_row < owner, up, my_col)
        targets = sum(when.astype(jnp.int32) for when in (to_next, to_prev, to_up, to_down))

        @pl.when(targets > 0)
        def _():
            pl.semaphore_wait(barrier, targets)

    def along_row(k):
        return pltpu.make_async_remote_copy(
            src_ref=flags,
            dst_ref=every.at[my_col, my_row],
            send_sem=row_send.at[k],
            recv_sem=row_recv.at[k],
            device_id=(lax.rem(my_row + k, n_row), my_col),
            device_id_type=MESH,
        )

    def along_col(k):
        return pltpu.make_async_remote_copy(
            src_ref=every.at[my_col],
            dst_ref=every.at[my_col],
            send_sem=col_send.at[k],
            recv_sem=col_recv.at[k],
            device_id=(my_row, lax.rem(my_col + k, n_col)),
            device_id_type=MESH,
        )

    if with_flags:
        own = pltpu.make_async_copy(flags, every.at[my_col, my_row], local)
        own.start()
        for k in range(1, n_row):
            along_row(k).start()

    def copy(src, dst, c, send, recv, row, col):
        part = pl.ds(c * span, span)
        return pltpu.make_async_remote_copy(
            src_ref=src.at[part],
            dst_ref=dst.at[part],
            send_sem=send.at[c],
            recv_sem=recv.at[c],
            device_id=(row, col),
            device_id_type=MESH,
        )

    def a_copies(src, c):
        return (
            (to_next, copy(src, a_dst, c, a_next, a_recv, my_row, nxt)),
            (to_prev, copy(src, a_dst, c, a_prev, a_recv, my_row, prv)),
        )

    def b_copies(src, c):
        return (
            (to_up, copy(src, b_dst, c, b_up, b_recv, up, my_col)),
            (to_down, copy(src, b_dst, c, b_down, b_recv, down, my_col)),
        )

    def start(copies):
        for when, one in copies:

            @pl.when(when)
            def _():
                one.start()

    @pl.when(b_root)
    def _():
        @pl.loop(0, CHUNKS)
        def _(c):
            start(b_copies(b_src, c))

    @pl.when(a_root)
    def _():
        @pl.loop(0, CHUNKS)
        def _(c):
            start(a_copies(a_src, c))

    def pass_a(c):
        @pl.when(jnp.logical_not(a_root))
        def _():
            copies = a_copies(a_dst, c)
            copies[0][1].wait_recv()
            start(copies)

    def pass_b(c):
        @pl.when(jnp.logical_not(b_root))
        def _():
            copies = b_copies(b_dst, c)
            copies[0][1].wait_recv()
            start(copies)

    if with_flags:
        own.wait()
        for k in range(1, n_row):
            along_row(k).wait_recv()
        for k in range(1, n_col):
            along_col(k).start()

    lag = 2

    @pl.loop(0, CHUNKS)
    def _(c):
        pass_b(c)

        @pl.when((c >= lag) & (c < lag + CHUNKS // 2))
        def _():
            pass_a(2 * (c - lag))
            pass_a(2 * (c - lag) + 1)

    @pl.loop(0, CHUNKS)
    def _(c):
        for when, one in a_copies(a_dst, c) + b_copies(b_dst, c):

            @pl.when(when)
            def _():
                one.wait_send()

    if with_flags:
        for k in range(1, n_row):
            along_row(k).wait_send()
        for k in range(1, n_col):
            along_col(k).wait()


def spread(root, owner, n_row, n_col, a_src, b_src, flags=None):
    shapes = [jax.ShapeDtypeStruct(x.shape, x.dtype) for x in (a_src, b_src)]
    operands = [a_src, b_src]
    sems = [pltpu.SemaphoreType.DMA((CHUNKS,))] * 6
    if flags is not None:
        operands.append(flags)
        shapes.append(jax.ShapeDtypeStruct((n_col, n_row) + flags.shape, flags.dtype))
        sems += [pltpu.SemaphoreType.DMA] + [pltpu.SemaphoreType.DMA((n,)) for n in (n_row, n_row, n_col, n_col)]
    return pl.pallas_call(
        functools.partial(spread_kernel, root, owner, n_row, n_col, flags is not None),
        out_shape=tuple(shapes),
        in_specs=[ANY] * len(operands),
        out_specs=(ANY,) * len(shapes),
        scratch_shapes=sems,
        compiler_params=pltpu.CompilerParams(
            collective_id=root + (n_col if flags is None else 0), has_side_effects=True
        ),
        name=f"spread_{root}" if flags is None else f"spread_flags_{root}",
    )(*operands)


def product_kernel(
    tile_rows, panel, tile_cols, ratio, block, sections, a_flags, b_flags, slots, filled,
    a_mine, b0_mine, b1_mine, a0, a1, b0, b1, out, a_full, b_full, done, zero, sem, out_sem,
):
    my_row, my_col = lax.axis_index("row"), lax.axis_index("col")
    zero[...] = jnp.zeros_like(zero)
    slot_count = tile_rows * tile_cols

    def fill(flags, s, mine, got, is_mine, full, rows, cols, first_p, first_q):
        def run(src):
            def lap(p, rank):
                for q in range(cols):
                    here = flags[s, p * cols + q]
                    spot = tile_at(full, first_p + p, first_q + q)

                    @pl.when(here == 1)
                    def _():
                        pltpu.make_async_copy(src.at[rank], spot, sem).start()

                    @pl.when(here == 0)
                    def _():
                        spot[...] = jnp.zeros((TILE, TILE), full.dtype)

                    rank = rank + here
                return rank

            return lax.fori_loop(0, rows, lap, jnp.int32(0))

        return lax.cond(is_mine, lambda: run(mine), lambda: run(got))

    total = jnp.int32(0)
    for s, got_a, mine_b, got_b in ((0, a0, b0_mine, b0), (1, a1, b1_mine, b1)):
        total += fill(a_flags, s, a_mine, got_a, sections[s] == my_col, a_full, tile_rows, panel, 0, s * panel)
        total += fill(
            b_flags, s, mine_b, got_b, sections[s] // ratio == my_row, b_full, panel, tile_cols, s * panel, 0
        )

    @pl.loop(filled[0], slot_count)
    def _(k):
        pltpu.make_async_copy(zero, tile_at(out, k // tile_cols, lax.rem(k, tile_cols)), out_sem).start()

    @pl.loop(0, total)
    def _(i):
        pltpu.make_async_copy(a_mine.at[0], tile_at(a_full, 0, 0), sem).wait()

    across = tile_cols // block
    down = tile_rows // block

    @pl.loop(0, down)
    def _(i):
        rows = pl.ds(pl.multiple_of(i * block * TILE, block * TILE), block * TILE)

        @pl.loop(0, across)
        def _(j):
            cols = pl.ds(pl.multiple_of(j * block * TILE, block * TILE), block * TILE)
            done[rows, cols] = jnp.dot(
                a_full[rows, :], b_full[:, cols], preferred_element_type=jnp.float32
            ).astype(done.dtype)

        @pl.loop(0, block)
        def _(r):
            p = i * block + r
            for q in range(tile_cols):
                slot = slots[p * tile_cols + q]

                @pl.when(slot >= 0)
                def _():
                    pltpu.make_async_copy(
                        tile_at(done, p, q),
                        tile_at(out, lax.div(slot, tile_cols), lax.rem(slot, tile_cols)),
                        out_sem,
                    ).start()

    pltpu.make_async_copy(done, out, out_sem).wait()


def shards(n_row, n_col, a_matrix, a_flags, b_matrix, b_flags, sections):
    tile_rows, panel = a_flags.shape
    tile_cols = b_flags.shape[1]
    ratio = n_col // n_row
    dtype = a_matrix.dtype
    my_row, my_col = lax.axis_index("row"), lax.axis_index("col")

    tiles = jax.ShapeDtypeStruct((MOST, TILE, TILE), dtype)
    a_mine, b0_mine, b1_mine = pl.pallas_call(
        functools.partial(pack_kernel, tile_rows, panel, tile_cols, ratio),
        out_shape=(tiles, tiles, tiles),
        in_specs=[SMEM, SMEM, SMEM, ANY, ANY],
        out_specs=(VMEM, VMEM, VMEM),
        scratch_shapes=[pltpu.SemaphoreType.DMA],
        name="pack",
    )(sections, a_flags, b_flags, a_matrix, b_matrix)

    flags = jnp.concatenate([a_flags, b_flags], axis=1)
    flags = jnp.pad(flags, ((0, 0), (0, -flags.shape[1] % TILE)))
    got = []
    for s, b_mine in ((0, b0_mine), (1, b1_mine)):
        operands = (a_mine, b_mine) if s else (a_mine, b_mine, flags)
        branches = [functools.partial(spread, t, t // ratio, n_row, n_col) for t in range(n_col)]
        got.append(lax.switch(sections[s], branches, *operands))
    every = got[0][2]

    own_a, own_b = [], []
    common = jnp.zeros((n_row, n_col, tile_rows, tile_cols), jnp.float32)
    for s in range(SECTIONS):
        section = sections[s]
        a_part = lax.dynamic_index_in_dim(every, section, 0, keepdims=False)[:, :, :panel]
        b_part = lax.dynamic_index_in_dim(every, section // ratio, 1, keepdims=False)
        b_part = lax.dynamic_slice_in_dim(b_part, section % ratio * panel, panel, 1)[:, :, panel : panel + tile_cols]
        own_a.append(lax.dynamic_index_in_dim(a_part, my_row, 0, keepdims=False).reshape(-1))
        own_b.append(lax.dynamic_index_in_dim(b_part, my_col, 0, keepdims=False).reshape(-1))
        common = common + jnp.einsum(
            "rpk,ckq->rcpq", a_part.astype(jnp.bfloat16), b_part.astype(jnp.bfloat16),
            preferred_element_type=jnp.float32,
        )
    occupied = (common > 0.5).astype(jnp.int32)
    counts = jnp.sum(occupied, axis=(2, 3)).reshape(-1)
    me = my_row * n_col + my_col
    offset = jnp.sum(jnp.where(jnp.arange(n_row * n_col) < me, counts, 0))
    own = occupied[my_row, my_col].reshape(-1)
    filled = jnp.sum(own)
    slots = jnp.where(own == 1, jnp.cumsum(own) - 1, -1).astype(jnp.int32)

    packed = pl.pallas_call(
        functools.partial(product_kernel, tile_rows, panel, tile_cols, ratio, 4),
        out_shape=jax.ShapeDtypeStruct((tile_rows * TILE, tile_cols * TILE), dtype),
        in_specs=[SMEM] * 5 + [ANY] * 7,
        out_specs=ANY,
        scratch_shapes=[
            pltpu.VMEM((tile_rows * TILE, SECTIONS * panel * TILE), dtype),
            pltpu.VMEM((SECTIONS * panel * TILE, tile_cols * TILE), dtype),
            pltpu.VMEM((tile_rows * TILE, tile_cols * TILE), dtype),
            pltpu.VMEM((TILE, TILE), dtype),
            pltpu.SemaphoreType.DMA,
            pltpu.SemaphoreType.DMA,
        ],
        compiler_params=pltpu.CompilerParams(vmem_limit_bytes=48 * 1024 * 1024),
        name="product",
    )(
        sections, jnp.stack(own_a), jnp.stack(own_b), slots, filled.reshape(1),
        a_mine, b0_mine, b1_mine, got[0][0], got[1][0], got[0][1], got[1][1],
    )
    slot_ids = jnp.arange(tile_rows * tile_cols, dtype=jnp.int32)
    places = jnp.where(slot_ids < filled, offset + slot_ids, -1).astype(jnp.int32)
    return packed, places.reshape(tile_rows, tile_cols)


def solution(mesh):
    return jax.shard_map(
        functools.partial(shards, mesh.shape["row"], mesh.shape["col"]),
        mesh=mesh,
        in_specs=(P("row", "col"), P("row", "col"), P("row", "col"), P("row", "col"), P()),
        out_specs=(P("row", "col"), P("row", "col")),
        check_vma=False,
    )
```

profile of v0, /device:TPU:2, one launch (start us, length us, event | category | flops | bytes accessed | tf_op | source)
XLA Modules:
  0.0 172.5 jit_solution(543405050171928666)
XLA Ops:
  0.6 1.3 fusion.22
  11.1 0.8 copy.21.a_flags
  11.8 0.0 copy-start.1
  11.8 0.8 pad_add_fusion
  12.6 0.0 copy-done.1
  12.6 2.9 %pack.1 = (bf16[64,128,128]{2,1,0:T(8,128)(2,1)S(1)}, bf16[64,128,128]{2,1,0:T(8,128)(2,1)}, bf16[64,128,128]{2,1,0:T(8,128)(2,1)}) custom-call(s32[2]{0:T(128)} %sections.3, s32[16,8]{1,0:T(8,128)} %copy-done.1, s32[16,16]{1,0:T(8,128)} %b_flags.1, bf16[2048,1024]{1,0:T(8,128)(2,1)} %a.1, bf16[2048,2048]{1,0:T(8,128)(2,1)} %b.1), custom_call_target="tpu_custom_call" | custom-call | tf_op jit(solution)/shard_map/pack/pallas_call | solution.py:330
  15.6 62.6 %conditional.3 = ((bf16[64,128,128]{2,1,0:T(8,128)(2,1)}, bf16[64,128,128]{2,1,0:T(8,128)(2,1)})) conditional(s32[]{:T(128)} %clamp.23, (bf16[64,128,128]{2,1,0:T(8,128)(2,1)S(1)}, bf16[64,128,128]{2,1,0:T(8,128)(2,1)}) %tuple.57, (bf16[64,128,128]{2,1,0:T(8,128)(2,1)S(1)}, ...), branch_computations={%region_11.12_spmd, %region_12.13_spmd, %region_13.14_spmd, %regio... | conditional | bytes 8 | solution.py:345
  15.6 62.5 %spread_4.1 = (bf16[64,128,128]{2,1,0:T(8,128)(2,1)}, bf16[64,128,128]{2,1,0:T(8,128)(2,1)}) custom-call(bf16[64,128,128]{2,1,0:T(8,128)(2,1)S(1)} %get-tuple-element.112.refs_0_, bf16[64,128,128]{2,1,0:T(8,128)(2,1)} %get-tuple-element.113.refs_1_), custom_call_target="tpu_custom_call" | custom-call | tf_op jit(solution)/shard_map/cond/branch_4_fun/spread_4/pallas_call | solution.py:233
  78.1 56.5 %conditional.2 = ((bf16[64,128,128]{2,1,0:T(8,128)(2,1)}, bf16[64,128,128]{2,1,0:T(8,128)(2,1)}, s32[8,4,16,128]{3,2,1,0:T(8,128)S(1)})) conditional(s32[]{:T(128)} %clamp.22, (bf16[64,128,128]{2,1,0:T(8,128)(2,1)S(1)}, bf16[64,128,128]{2,1,0:T(8,128)(2,1)}, s32[16,128]{1,0:T(8,128)S(1)}) %tuple.56, ...), branch_computations={%region_0.1_spmd, %region_1.2_spmd, %region_2.3_spmd, %region_3.4_... | conditional | bytes 8 | solution.py:345
  78.2 56.5 %spread_flags_5.1 = (bf16[64,128,128]{2,1,0:T(8,128)(2,1)}, bf16[64,128,128]{2,1,0:T(8,128)(2,1)}, s32[8,4,16,128]{3,2,1,0:T(8,128)S(1)}) custom-call(bf16[64,128,128]{2,1,0:T(8,128)(2,1)S(1)} %get-tuple-element.95.refs_0_, bf16[64,128,128]{2,1,0:T(8,128)(2,1)} %get-tuple-element.96.refs_1_, s32[16,128]{1,0:T(8,128)S(1)} %get-tuple-element.97.refs_2_), custom_call_target="tpu_custom_call" | custom-call | tf_op jit(solution)/shard_map/cond/branch_5_fun/spread_flags_5/pallas_call | solution.py:233
  134.7 0.0 copy-start
  134.7 0.1 slice.37
  134.8 0.1 stack_reshape.14
  134.9 0.1 slice.38
  135.0 0.1 stack_reshape.15
  135.1 0.1 copy.23
  135.2 0.3 fusion.8
  135.5 0.1 copy.24
  135.6 0.1 stack_reshape.12
  135.7 0.1 copy.25
  135.8 0.3 fusion.4
  136.2 0.1 copy.26
  136.2 0.1 stack_reshape.13
  136.3 0.7 fusion.6
  137.0 0.6 fusion.17
  137.7 0.7 dynamic-slice_reduce_fusion
  138.4 0.1 copy.27
  138.4 0.1 eq.10
  138.5 1.9 %add_select_fusion = s32[16,16]{1,0:T(8,128)} fusion(s32[]{:T(128)} %fusion.17, s32[]{:T(128)} %dynamic-slice_reduce_fusion), kind=kLoop, calls=%fused_computation.19 | loop fusion | flops 1280 | bytes 1032 | tf_op jit(solution)/shard_map/jit(_where)/select_n | solution.py:389
  140.4 0.1 copy.28
  140.5 0.1 reshape.37
  140.6 0.3 reduce-window.9
  140.9 0.1 slice.33
  141.0 0.1 slice_reduce_fusion
  141.1 0.1 bitcast_select_fusion.1.slots
  141.2 0.0 copy-done
  141.2 31.3 %product.1 = bf16[2048,2048]{1,0:T(8,128)(2,1)} custom-call(s32[2]{0:T(128)S(1)} %copy-done, s32[2,128]{1,0:T(2,128)S(1)} %get-tuple-element.146.a_flags, s32[2,128]{1,0:T(2,128)S(1)} %get-tuple-element.147.b_flags, s32[256]{0:T(256)S(1)} %bitcast_select_fusion.1.slots, s32[1]{0:T(128)} %bitcast.14.filled, ...), custom_call_target="tpu_custom_call" | custom-call | tf_op jit(solution)/shard_map/product/pallas_call | solution.py:369
  (13 shorter events, 0.2 us)
Async XLA Ops:
  11.8 0.8 copy-start.1
  134.7 6.5 %copy-start = (s32[2]{0:T(128)S(1)}, s32[2]{0:T(128)}, u32[]{:S(2)}) copy-start(s32[2]{0:T(128)} %sections.3) | copy-start | bytes 28
where the time goes:
time: 173 us; the launch traced here: 172 us
  Pallas kernels  153 us (88%)
  between operations  9.9 us (6%)
  other arithmetic  5.07 us (3%)
  local copies, waits for them, and re-layouts  3.58 us (2%)
    pallas_call x2, Pallas kernels, spread(): pl.pallas_call(functools.partial(spread_kernel, root, owner, n_row, n_col...  119 us
    pallas_call x1, Pallas kernels, shards(): pl.pallas_call(functools.partial(product_kernel, tile_rows, panel, tile_c...  31.3 us

commit v1 on v0

v1 whole, which is shorter than its diff:
```python
import functools

import jax
import jax.numpy as jnp
from jax import lax
from jax.experimental import pallas as pl
from jax.experimental.pallas import tpu as pltpu
from jax.sharding import PartitionSpec as P

TILE = 128
SECTIONS = 2
MOST = 64
HALF = MOST // 2
SPAN = 2
STEPS = MOST // SPAN
A_SPAN = 4
A_STEPS = HALF // A_SPAN
BLOCK = 512
MESH = pl.DeviceIdType.MESH
ANY = pl.BlockSpec(memory_space=pl.ANY)
SMEM = pl.BlockSpec(memory_space=pltpu.SMEM)
VMEM = pl.BlockSpec(memory_space=pltpu.VMEM)


def tile_at(ref, p, q):
    rows = pl.ds(pl.multiple_of(p * TILE, TILE), TILE)
    cols = pl.ds(q * TILE if isinstance(q, int) else pl.multiple_of(q * TILE, TILE), TILE)
    return ref.at[rows, cols]


def pack_kernel(tile_rows, panel, tile_cols, ratio, sections, a_flags, b_flags, a_vec, b_vec, a, b, a_out, b_out, flags, sem):
    def gather(occupied, src, out, rows, cols, first):
        def lap(p, rank):
            for q in range(cols):
                here = occupied[first + p, q]

                @pl.when(here == 1)
                def _():
                    pltpu.make_async_copy(tile_at(src, first + p, q), out.at[rank], sem).start()

                rank = rank + here
            return rank

        return lax.fori_loop(0, rows, lap, jnp.int32(0))

    total = jnp.int32(0)
    my_row, my_col = lax.axis_index("row"), lax.axis_index("col")
    mine_a = (sections[0] == my_col) | (sections[1] == my_col)
    for s in range(SECTIONS):
        first = lax.rem(sections[s], ratio) * panel
        total += lax.cond(
            sections[s] // ratio == my_row,
            lambda: gather(b_flags, b, b_out.at[s], panel, tile_cols, first),
            lambda: jnp.int32(0),
        )
    total += lax.cond(mine_a, lambda: gather(a_flags, a, a_out, tile_rows, panel, 0), lambda: jnp.int32(0))

    flags[...] = jnp.zeros_like(flags)
    ahead = tile_rows // panel
    for i in range(ahead):
        flags[i, :, 0:panel] = a_vec[i * panel : (i + 1) * panel, :]
    for i in range(ratio):
        flags[ahead + i, :, 0:tile_cols] = b_vec[i * panel : (i + 1) * panel, :]

    @pl.loop(0, total)
    def _(i):
        pltpu.make_async_copy(tile_at(a, 0, 0), a_out.at[0], sem).wait()


def comm_kernel(
    n_row, n_col, tile_rows, panel, tile_cols, ratio,
    sections, own_a, own_b, flags, done, meta,
    every, staged, table, occ, swapped, held, a0, a1, b0, b1, a_full, b_full, acc, stages,
    local, row_send, row_recv, col_send, col_recv,
    up_send, up_recv, down_send, down_recv, core_send, core_recv, stage_send, stage_recv, last_send, last_recv,
):
    my_row, my_col = lax.axis_index("row"), lax.axis_index("col")
    bits = n_col.bit_length() - 1
    ahead = tile_rows // panel
    side = lax.rem(my_col, 2)
    partner = my_col + 1 - 2 * side
    above = jnp.minimum(my_row + 1, n_row - 1)
    below = jnp.maximum(my_row - 1, 0)
    b_parts, a_parts = (b0, b1), (a0, a1)
    tags = [sections[s] for s in range(SECTIONS)]
    owners = [lax.div(tag, ratio) for tag in tags]

    def flip(bit):
        on = lax.rem(lax.div(my_col, 1 << bit), 2)
        return my_col + (1 << bit) - 2 * on * (1 << bit)

    barrier = pltpu.get_barrier_semaphore()
    for k in range(1, n_row):
        pl.semaphore_signal(barrier, inc=1, device_id=(lax.rem(my_row + k, n_row), my_col), device_id_type=MESH)
    for k in range(1, n_col):
        pl.semaphore_signal(barrier, inc=1, device_id=(my_row, lax.rem(my_col + k, n_col)), device_id_type=MESH)
    pl.semaphore_wait(barrier, n_row + n_col - 2)

    def send(src, dst, send_sem, recv_sem, row, col):
        return pltpu.make_async_remote_copy(
            src_ref=src, dst_ref=dst, send_sem=send_sem, recv_sem=recv_sem,
            device_id=(row, col), device_id_type=MESH,
        )

    def along_row(k):
        return send(
            flags, every.at[my_col, my_row], row_send.at[k], row_recv.at[k], lax.rem(my_row + k, n_row), my_col
        )

    def along_col(k):
        return send(
            every.at[my_col], every.at[my_col], col_send.at[k], col_recv.at[k], my_row, lax.rem(my_col + k, n_col)
        )

    def up(s, c, src=None):
        part = pl.ds(c * SPAN, SPAN)
        i = s * STEPS + c
        src = b_parts[s] if src is None else src
        return send(src.at[part], b_parts[s].at[part], up_send.at[i], up_recv.at[i], above, my_col)

    def down(s, c, src=None):
        part = pl.ds(MOST + c * SPAN, SPAN)
        i = s * STEPS + c
        src = b_parts[s].at[part] if src is None else src.at[pl.ds(c * SPAN, SPAN)]
        return send(src, b_parts[s].at[part], down_send.at[i], down_recv.at[i], below, my_col)

    def core_swap():
        return send(
            own_a.at[pl.ds((1 - side) * HALF, HALF)], swapped, core_send, core_recv, my_row, partner
        )

    def stage(bit, j):
        src = held if bit == 1 else stages.at[bit - 2]
        part = pl.ds(j * A_SPAN, A_SPAN)
        return send(
            src.at[part], stages.at[bit - 1, part], stage_send.at[bit - 1, j], stage_recv.at[bit - 1, j],
            my_row, flip(bit),
        )

    def last(s, j):
        part = pl.ds(side * HALF + j * A_SPAN, A_SPAN)
        i = s * A_STEPS + j
        return send(a_parts[s].at[part], a_parts[s].at[part], last_send.at[i], last_recv.at[i], my_row, partner)

    own = pltpu.make_async_copy(flags, every.at[my_col, my_row], local)
    own.start()
    for k in range(1, n_row):
        along_row(k).start()
    core_swap().start()

    @pl.when(my_row == 0)
    def _():
        for s in range(SECTIONS):

            @pl.loop(0, STEPS)
            def _(c):
                up(s, c, own_b.at[s]).start()

    @pl.when(my_row == n_row - 1)
    def _():
        for s in range(SECTIONS):

            @pl.loop(0, STEPS)
            def _(c):
                down(s, c, own_b.at[s]).start()

    own.wait()
    for k in range(1, n_row):
        along_row(k).wait_recv()
    for k in range(1, n_col):
        along_col(k).start()

    core_swap().wait_recv()
    for s in range(SECTIONS):
        mine = tags[s] == my_col

        @pl.loop(0, HALF)
        def _(k):
            held[s * HALF + k] = jnp.where(mine, own_a[side * HALF + k], swapped[k])

    @pl.loop(0, SECTIONS * A_STEPS)
    def _(j):
        stage(1, j).start()

    def hop(s, c):
        inject = owners[s] == my_row

        @pl.when(my_row > 0)
        def _():
            up(s, c).wait_recv()
            for k in range(SPAN):
                b_parts[s][c * SPAN + k] = jnp.where(inject, own_b[s, c * SPAN + k], b_parts[s][c * SPAN + k])

            @pl.when(my_row < n_row - 1)
            def _():
                up(s, c).start()

        @pl.when(my_row < n_row - 1)
        def _():
            down(s, c).wait_recv()
            for k in range(SPAN):
                spot = MOST + c * SPAN + k
                b_parts[s][spot] = jnp.where(inject, own_b[s, c * SPAN + k], b_parts[s][spot])

            @pl.when(my_row > 0)
            def _():
                down(s, c).start()

    def pass_a(bit, j):
        stage(bit, j).wait_recv()
        final = bit == bits - 1
        for s in range(SECTIONS):

            @pl.when((j >= s * A_STEPS) & (j < (s + 1) * A_STEPS))
            def _():
                near = lax.div(tags[s], 1 << bit) == lax.div(my_col, 1 << bit)
                for k in range(A_SPAN):
                    i = j * A_SPAN + k
                    before = held[i] if bit == 1 else stages[bit - 2, i]
                    got = jnp.where(near, before, stages[bit - 1, i])
                    if final:
                        a_parts[s][side * HALF + i - s * HALF] = got
                    else:
                        stages[bit - 1, i] = got
                if final:
                    last(s, j - s * A_STEPS).start()

        if not final:
            stage(bit + 1, j).start()

    lag = 4

    def pass_all(i):
        for bit in range(1, bits):
            j2 = i - lag * bit

            @pl.when((j2 >= 0) & (j2 < 2 * SECTIONS * A_STEPS) & (lax.rem(j2, 2) == 0))
            def _():
                pass_a(bit, lax.div(j2, 2))

    def step(i, s):
        hop(s, i - s * STEPS)
        pass_all(i)

    first = 4

    @pl.loop(0, first)
    def _(i):
        step(i, 0)

    for k in range(1, n_col):
        along_col(k).wait_recv()

    for s in range(SECTIONS):
        for i in range(ahead):
            staged[s, i] = every[tags[s], my_row, i]
        staged[s, ahead] = every[my_col, owners[s], ahead + lax.rem(tags[s], ratio)]
    tables = pltpu.make_async_copy(staged, table, local)
    tables.start()

    sides = []
    for s in range(SECTIONS):
        rows = [every[tags[s], r, i] for r in range(n_row) for i in range(ahead)]
        sides.append(jnp.concatenate(rows, axis=0).astype(jnp.float32)[:, 0:panel])
    blocks = lax.broadcasted_iota(jnp.int32, (n_row * tile_rows, TILE), 0) // tile_rows * n_col
    me = my_row * n_col + my_col
    lower = jnp.zeros((n_row * tile_rows, TILE), jnp.float32)
    chosen = jnp.zeros((n_row * tile_rows, TILE), jnp.float32)
    for c in range(n_col):
        common = jnp.zeros((n_row * tile_rows, TILE), jnp.float32)
        for s in range(SECTIONS):
            tile_flags = every[c, owners[s], ahead + lax.rem(tags[s], ratio)].astype(jnp.float32)
            common += jnp.dot(sides[s], tile_flags, preferred_element_type=jnp.float32)
        occupied = jnp.where(common > 0.5, 1.0, 0.0)
        lower += jnp.where(blocks + c < me, occupied, 0.0)
        chosen += jnp.where(my_col == c, occupied, 0.0)
    occ[...] = chosen
    offset = jnp.sum(jnp.sum(lower, axis=1, keepdims=True), axis=0, keepdims=True)
    meta[0:tile_rows] = occ[pl.ds(pl.multiple_of(my_row * tile_rows, tile_rows), tile_rows)].astype(jnp.int32)
    meta[tile_rows:] = jnp.broadcast_to(offset, (8, TILE)).astype(jnp.int32)
    tables.wait()

    @pl.loop(first, STEPS)
    def _(i):
        step(i, 0)

    def put(ref, p, cols, rank, flag_at, part, base):
        for q in range(cols):
            here = flag_at(q)
            spot = tile_at(ref, p, q)
            got = part[base + jnp.minimum(rank, MOST - 1)]
            spot[...] = jnp.where(here == 1, got, jnp.zeros_like(got))
            rank = rank + here
        return rank

    def spread_a(s, p, rank):
        return put(a_full, p, panel, rank, lambda q: table[s, lax.div(p, panel), lax.rem(p, panel), q], a_parts[s], 0)

    def spread_b(s, p, rank):
        base = jnp.where((owners[s] >= my_row) & (my_row < n_row - 1), MOST, 0)
        return put(b_full, p, tile_cols, rank, lambda q: table[s, ahead, p, q], b_parts[s], base)

    for j in range(A_STEPS):
        last(0, j).wait_recv()

    def fill_first(c, ranks):
        rank_a, rank_b = ranks
        step(STEPS + c, 1)
        for k in range(tile_rows // panel):
            rank_a = spread_a(0, c * (tile_rows // panel) + k, rank_a)
        rank_b = spread_b(0, c, rank_b)
        return rank_a, rank_b

    lax.fori_loop(0, panel, fill_first, (jnp.int32(0), jnp.int32(0)))

    across = tile_cols * TILE // BLOCK
    down_blocks = tile_rows * TILE // BLOCK

    def block_of(j):
        rows = pl.ds(pl.multiple_of(lax.div(j, across) * BLOCK, BLOCK), BLOCK)
        cols = pl.ds(pl.multiple_of(lax.rem(j, across) * BLOCK, BLOCK), BLOCK)
        return rows, cols

    def product(j):
        rows, cols = block_of(j)
        return rows, cols, jnp.dot(a_full[rows, :], b_full[:, cols], preferred_element_type=jnp.float32)

    pieces = across * down_blocks

    @pl.loop(0, pieces)
    def _(j):
        step(STEPS + panel + j, 1)
        rows, cols, got = product(j)
        acc[rows, cols] = got

    @pl.loop(panel + pieces, STEPS - panel)
    def _(c):
        step(STEPS + c, 1)

    for j in range(A_STEPS):
        last(1, j).wait_recv()

    def fill_second(c, rank_a):
        step(2 * STEPS - panel + c, 1)
        for k in range(tile_rows // panel):
            rank_a = spread_a(1, c * (tile_rows // panel) + k, rank_a)
        return rank_a

    lax.fori_loop(0, panel, fill_second, jnp.int32(0))
    lax.fori_loop(0, panel, functools.partial(spread_b, 1), jnp.int32(0))

    @pl.loop(0, pieces)
    def _(j):
        rows, cols, got = product(j)
        done[rows, cols] = (acc[rows, cols] + got).astype(done.dtype)

    for k in range(1, n_row):
        along_row(k).wait_send()
    for k in range(1, n_col):
        along_col(k).wait_send()
    core_swap().wait_send()
    for s in range(SECTIONS):

        @pl.loop(0, A_STEPS)
        def _(j):
            last(s, j).wait_send()

        @pl.loop(0, STEPS)
        def _(c):
            @pl.when(my_row < n_row - 1)
            def _():
                up(s, c).wait_send()

            @pl.when(my_row > 0)
            def _():
                down(s, c).wait_send()

    for bit in range(1, bits):

        @pl.loop(0, SECTIONS * A_STEPS)
        def _(j):
            stage(bit, j).wait_send()


def final_kernel(tile_rows, tile_cols, meta, done, out, places, zero, sem):
    zero[...] = jnp.zeros_like(zero)

    def lap(p, rank):
        for q in range(tile_cols):
            here = meta[p, q]

            @pl.when(here == 1)
            def _():
                spot = tile_at(out, lax.div(rank, tile_cols), lax.rem(rank, tile_cols))
                pltpu.make_async_copy(tile_at(done, p, q), spot, sem).start()

            rank = rank + here
        return rank

    filled = lax.fori_loop(0, tile_rows, lap, jnp.int32(0))

    @pl.loop(filled, tile_rows * tile_cols)
    def _(k):
        pltpu.make_async_copy(zero, tile_at(out, lax.div(k, tile_cols), lax.rem(k, tile_cols)), sem).start()

    slot = lax.broadcasted_iota(jnp.int32, places.shape, 0) * tile_cols + lax.broadcasted_iota(jnp.int32, places.shape, 1)
    places[...] = jnp.where(slot < filled, meta[tile_rows, 0] + slot, -1)
    pltpu.make_async_copy(done, out, sem).wait()


def shards(n_row, n_col, a_matrix, a_flags, b_matrix, b_flags, sections):
    tile_rows, panel = a_flags.shape
    tile_cols = b_flags.shape[1]
    ratio = n_col // n_row
    dtype = a_matrix.dtype
    bits = n_col.bit_length() - 1
    ahead = tile_rows // panel

    def tiles(*lead):
        return lead + (TILE, TILE)

    own_a, own_b, flags = pl.pallas_call(
        functools.partial(pack_kernel, tile_rows, panel, tile_cols, ratio),
        out_shape=(
            jax.ShapeDtypeStruct(tiles(MOST), dtype),
            jax.ShapeDtypeStruct(tiles(SECTIONS, MOST), dtype),
            jax.ShapeDtypeStruct((ahead + ratio, panel, TILE), jnp.int32),
        ),
        in_specs=[SMEM, SMEM, SMEM, VMEM, VMEM, ANY, ANY],
        out_specs=(VMEM, VMEM, VMEM),
        scratch_shapes=[pltpu.SemaphoreType.DMA],
        compiler_params=pltpu.CompilerParams(vmem_limit_bytes=16 * 1024 * 1024),
        name="pack",
    )(sections, a_flags, b_flags, a_flags, b_flags, a_matrix, b_matrix)

    size = (tile_rows * TILE, tile_cols * TILE)
    dma = pltpu.SemaphoreType.DMA
    done, meta = pl.pallas_call(
        functools.partial(comm_kernel, n_row, n_col, tile_rows, panel, tile_cols, ratio),
        out_shape=(jax.ShapeDtypeStruct(size, dtype), jax.ShapeDtypeStruct((tile_rows + 8, TILE), jnp.int32)),
        in_specs=[SMEM, VMEM, VMEM, VMEM],
        out_specs=(VMEM, VMEM),
        scratch_shapes=[
            pltpu.VMEM((n_col, n_row, ahead + ratio, panel, TILE), jnp.int32),
            pltpu.VMEM((SECTIONS, ahead + 1, panel, TILE), jnp.int32),
            pltpu.SMEM((SECTIONS, ahead + 1, panel, TILE), jnp.int32),
            pltpu.VMEM((n_row * tile_rows, TILE), jnp.float32),
            pltpu.VMEM(tiles(HALF), dtype),
            pltpu.VMEM(tiles(MOST), dtype),
            pltpu.VMEM(tiles(MOST), dtype),
            pltpu.VMEM(tiles(MOST), dtype),
            pltpu.VMEM(tiles(2 * MOST), dtype),
            pltpu.VMEM(tiles(2 * MOST), dtype),
            pltpu.VMEM((tile_rows * TILE, panel * TILE), dtype),
            pltpu.VMEM((panel * TILE, tile_cols * TILE), dtype),
            pltpu.VMEM(size, jnp.float32),
            pltpu.VMEM(tiles(bits - 1, MOST), dtype),
            dma, dma((n_row,)), dma((n_row,)), dma((n_col,)), dma((n_col,)),
            dma((SECTIONS * STEPS,)), dma((SECTIONS * STEPS,)), dma((SECTIONS * STEPS,)), dma((SECTIONS * STEPS,)),
            dma, dma,
            dma((bits - 1, SECTIONS * A_STEPS)), dma((bits - 1, SECTIONS * A_STEPS)),
            dma((SECTIONS * A_STEPS,)), dma((SECTIONS * A_STEPS,)),
        ],
        compiler_params=pltpu.CompilerParams(
            collective_id=0, has_side_effects=True, vmem_limit_bytes=67043328
        ),
        name="exchange",
    )(sections, own_a, own_b, flags)

    return pl.pallas_call(
        functools.partial(final_kernel, tile_rows, tile_cols),
        out_shape=(jax.ShapeDtypeStruct(size, dtype), jax.ShapeDtypeStruct((tile_rows, tile_cols), jnp.int32)),
        in_specs=[SMEM, VMEM],
        out_specs=(ANY, VMEM),
        scratch_shapes=[pltpu.VMEM((TILE, TILE), dtype), pltpu.SemaphoreType.DMA],
        compiler_params=pltpu.CompilerParams(vmem_limit_bytes=16 * 1024 * 1024),
        name="compact",
    )(meta, done)


def solution(mesh):
    return jax.shard_map(
        functools.partial(shards, mesh.shape["row"], mesh.shape["col"]),
        mesh=mesh,
        in_specs=(P("row", "col"), P("row", "col"), P("row", "col"), P("row", "col"), P()),
        out_specs=(P("row", "col"), P("row", "col")),
        check_vma=False,
    )
```

time: 173 us -> 512 us (2.96)
  the two profiles are of different devices: /device:TPU:2 before, /device:TPU:0 now
where the time goes in v1:
time: 512 us; the launch traced here: 511 us
  Pallas kernels  494 us (96%)
  local copies, waits for them, and re-layouts  15.7 us (3%)
    pallas_call x1, Pallas kernels, shards(): pl.pallas_call(functools.partial(comm_kernel, n_row, n_col, tile_rows, pa...  486 us
    unnamed x19, local copies, waits for them, and re-layouts  15.7 us

profile of v1, /device:TPU:0, one launch (start us, length us, event | category | flops | bytes accessed | tf_op | source)
XLA Modules:
  0.0 510.9 jit_solution(12510476164904188560)
XLA Ops:
  0.6 0.8 copy.7.a_flags.a_vec
  1.4 0.0 copy-start
  1.4 3.4 copy-done
  4.8 0.0 copy-start.3
  4.8 2.2 copy-done.3
  7.0 0.0 copy-start.5
  7.0 0.7 copy-done.5
  7.7 0.0 copy-start.8
  7.7 0.7 copy-done.8
  8.3 4.2 pack.1
  12.5 0.0 copy-start.2
  12.5 2.0 copy-done.2
  14.5 0.0 copy-start.4
  14.5 1.4 copy-done.4
  15.9 0.0 copy-start.6
  15.9 0.6 copy-done.6
  16.5 485.8 %exchange.1 = (bf16[2048,2048]{1,0:T(8,128)(2,1)}, s32[24,128]{1,0:T(8,128)}) custom-call(s32[2]{0:T(128)} %sections.3, bf16[64,128,128]{2,1,0:T(8,128)(2,1)} %copy-done.4, bf16[2,64,128,128]{3,2,1,0:T(8,128)(2,1)} %copy-done.2, s32[4,8,128]{2,1,0:T(8,128)} %copy-done.6), custom_call_target="tpu_custom_call" | custom-call | tf_op jit(solution)/shard_map/exchange/pallas_call | solution.py:438
  502.3 0.0 copy-start.1
  502.3 3.4 copy-done.1
  505.7 0.0 copy-start.7
  505.7 0.7 copy-done.7
  506.4 4.5 compact.1
Async XLA Ops:
  1.4 3.4 copy-start
  4.8 2.2 copy-start.3
  7.0 0.7 copy-start.5
  7.7 0.7 copy-start.8
  12.5 2.0 copy-start.2
  14.5 1.4 copy-start.4
  15.9 0.6 copy-start.6
  502.3 3.4 copy-start.1
  505.7 0.7 copy-start.7

commit v2 on v1

v2 whole, which is shorter than its diff:
```python
import functools

import jax
import jax.numpy as jnp
from jax import lax
from jax.experimental import pallas as pl
from jax.experimental.pallas import tpu as pltpu
from jax.sharding import PartitionSpec as P

TILE = 128
SECTIONS = 2
MOST = 64
HALF = MOST // 2
SPAN = 2
STEPS = MOST // SPAN
A_SPAN = 4
A_STEPS = HALF // A_SPAN
BLOCK = 512
WINDOW = 6
SKEW = 3
MESH = pl.DeviceIdType.MESH
HBM = pl.BlockSpec(memory_space=pltpu.HBM)
SMEM = pl.BlockSpec(memory_space=pltpu.SMEM)
VMEM = pl.BlockSpec(memory_space=pltpu.VMEM)


def tile_at(ref, p, q):
    rows = pl.ds(pl.multiple_of(p * TILE, TILE), TILE)
    cols = pl.ds(q * TILE if isinstance(q, int) else pl.multiple_of(q * TILE, TILE), TILE)
    return ref.at[rows, cols]


def block_at(j):
    return pl.ds(pl.multiple_of(j * BLOCK, BLOCK), BLOCK)


def pack_kernel(
    tile_rows, panel, tile_cols, ratio, sections_in, a_flags_in, b_flags_in, a, b,
    a_out, b_out, flags, sections, a_flags, b_flags, a_vec, b_vec, sems, sem,
):
    moves = (
        (sections_in, sections), (b_flags_in, b_flags), (a_flags_in, a_flags), (a_flags_in, a_vec), (b_flags_in, b_vec)
    )
    loads = [pltpu.make_async_copy(src, dst, sems.at[i]) for i, (src, dst) in enumerate(moves)]
    for load in loads:
        load.start()
    flags[...] = jnp.zeros_like(flags)
    for load in loads:
        load.wait()

    def gather(occupied, src, out, rows, cols, first, turned):
        def lap(p, rank):
            for q in range(cols):
                here = occupied[q, p] if turned else occupied[first + p, q]

                @pl.when(here == 1)
                def _():
                    pltpu.make_async_copy(tile_at(src, first + p, q), out.at[rank], sem).start()

                rank = rank + here
            return rank

        return lax.fori_loop(0, rows, lap, jnp.int32(0))

    total = jnp.int32(0)
    my_row, my_col = lax.axis_index("row"), lax.axis_index("col")
    mine_a = (sections[0] == my_col) | (sections[1] == my_col)
    for s in range(SECTIONS):
        first = lax.rem(sections[s], ratio) * panel
        total += lax.cond(
            sections[s] // ratio == my_row,
            lambda: gather(b_flags, b, b_out.at[s], panel, tile_cols, first, False),
            lambda: jnp.int32(0),
        )
    total += lax.cond(mine_a, lambda: gather(a_flags, a, a_out, tile_rows, panel, 0, True), lambda: jnp.int32(0))

    flags[0, :, 0:tile_rows] = a_vec[...]
    for i in range(ratio):
        flags[1 + i, :, 0:tile_cols] = b_vec[i * panel : (i + 1) * panel, :]

    @pl.loop(0, total)
    def _(i):
        pltpu.make_async_copy(tile_at(a, 0, 0), a_out.at[0], sem).wait()


def comm_kernel(
    n_row, n_col, tile_rows, panel, tile_cols, ratio,
    sections_in, own_a, own_b, flags, acc0, acc1, a_full, b_full, meta,
    sections, every, staged, table, occ, swapped, held, a0, a1, b0, b1, stages,
    local, brief, row_send, row_recv, col_send, col_recv,
    up_send, up_recv, down_send, down_recv, core_send, core_recv, stage_send, stage_recv, last_send, last_recv,
):
    my_row, my_col = lax.axis_index("row"), lax.axis_index("col")
    bits = n_col.bit_length() - 1
    side = lax.rem(my_col, 2)
    partner = my_col + 1 - 2 * side
    above = jnp.minimum(my_row + 1, n_row - 1)
    below = jnp.maximum(my_row - 1, 0)
    b_parts, a_parts = (b0, b1), (a0, a1)

    def flip(bit):
        on = lax.rem(lax.div(my_col, 1 << bit), 2)
        return my_col + (1 << bit) - 2 * on * (1 << bit)

    choice = pltpu.make_async_copy(sections_in, sections, brief)
    choice.start()
    barrier = pltpu.get_barrier_semaphore()
    for k in range(1, n_row):
        pl.semaphore_signal(barrier, inc=1, device_id=(lax.rem(my_row + k, n_row), my_col), device_id_type=MESH)
    for k in range(1, n_col):
        pl.semaphore_signal(barrier, inc=1, device_id=(my_row, lax.rem(my_col + k, n_col)), device_id_type=MESH)
    pl.semaphore_wait(barrier, n_row + n_col - 2)

    def send(src, dst, send_sem, recv_sem, row, col):
        return pltpu.make_async_remote_copy(
            src_ref=src, dst_ref=dst, send_sem=send_sem, recv_sem=recv_sem,
            device_id=(row, col), device_id_type=MESH,
        )

    def along_row(k):
        return send(
            flags, every.at[my_col, my_row], row_send.at[k], row_recv.at[k], lax.rem(my_row + k, n_row), my_col
        )

    def along_col(k):
        return send(
            every.at[my_col], every.at[my_col], col_send.at[k], col_recv.at[k], my_row, lax.rem(my_col + k, n_col)
        )

    def up(s, c, src=None):
        part = pl.ds(c * SPAN, SPAN)
        i = s * STEPS + c
        src = b_parts[s] if src is None else src
        return send(src.at[part], b_parts[s].at[part], up_send.at[i], up_recv.at[i], above, my_col)

    def down(s, c, src=None):
        part = pl.ds(MOST + c * SPAN, SPAN)
        i = s * STEPS + c
        src = b_parts[s].at[part] if src is None else src.at[pl.ds(c * SPAN, SPAN)]
        return send(src, b_parts[s].at[part], down_send.at[i], down_recv.at[i], below, my_col)

    def core_swap():
        return send(
            own_a.at[pl.ds((1 - side) * HALF, HALF)], swapped, core_send, core_recv, my_row, partner
        )

    def stage(bit, j):
        src = held if bit == 1 else stages.at[bit - 2]
        part = pl.ds(j * A_SPAN, A_SPAN)
        return send(
            src.at[part], stages.at[bit - 1, part], stage_send.at[bit - 1, j], stage_recv.at[bit - 1, j],
            my_row, flip(bit),
        )

    def last(s, j):
        part = pl.ds(side * HALF + j * A_SPAN, A_SPAN)
        i = s * A_STEPS + j
        return send(a_parts[s].at[part], a_parts[s].at[part], last_send.at[i], last_recv.at[i], my_row, partner)

    own = pltpu.make_async_copy(flags, every.at[my_col, my_row], local)
    own.start()
    for k in range(1, n_row):
        along_row(k).start()
    core_swap().start()

    @pl.when(my_row == 0)
    def _():
        @pl.loop(0, WINDOW)
        def _(c):
            up(0, c, own_b.at[0]).start()

    @pl.when(my_row == n_row - 1)
    def _():
        @pl.loop(0, WINDOW)
        def _(c):
            down(0, c, own_b.at[0]).start()

    own.wait()
    for k in range(1, n_row):
        along_row(k).wait_recv()
    for k in range(1, n_col):
        along_col(k).start()

    choice.wait()
    tags = [sections[s] for s in range(SECTIONS)]
    owners = [lax.div(tag, ratio) for tag in tags]
    core_swap().wait_recv()
    for s in range(SECTIONS):
        mine = tags[s] == my_col

        @pl.loop(0, HALF)
        def _(k):
            held[s * HALF + k] = jnp.where(mine, own_a[side * HALF + k], swapped[k])

    @pl.loop(0, SECTIONS * A_STEPS)
    def _(j):
        stage(1, j).start()

    def parted(g, body):
        for s in range(SECTIONS):

            @pl.when((g >= s * STEPS) & (g < (s + 1) * STEPS))
            def _():
                body(s, g - s * STEPS)

    def feed(way, i):
        parted(i, lambda s, c: way(s, c).wait_send())
        parted(i + WINDOW, lambda s, c: way(s, c, own_b.at[s]).start())

    def take(way, first, onward, s, c):
        way(s, c).wait_recv()
        inject = owners[s] == my_row
        for k in range(SPAN):
            spot = first + c * SPAN + k
            b_parts[s][spot] = jnp.where(inject, own_b[s, c * SPAN + k], b_parts[s][spot])

        @pl.when(onward)
        def _():
            way(s, c).start()

    def hop(i):
        @pl.when(my_row == 0)
        def _():
            feed(up, i)

        @pl.when(my_row == n_row - 1)
        def _():
            feed(down, i)

        @pl.when(my_row > 0)
        def _():
            parted(i - SKEW * my_row, functools.partial(take, up, 0, my_row < n_row - 1))

        @pl.when(my_row < n_row - 1)
        def _():
            parted(i - SKEW * (n_row - 1 - my_row), functools.partial(take, down, MOST, my_row > 0))

    def pass_a(bit, j):
        stage(bit, j).wait_recv()
        final = bit == bits - 1
        for s in range(SECTIONS):

            @pl.when((j >= s * A_STEPS) & (j < (s + 1) * A_STEPS))
            def _():
                near = lax.div(tags[s], 1 << bit) == lax.div(my_col, 1 << bit)
                for k in range(A_SPAN):
                    i = j * A_SPAN + k
                    before = held[i] if bit == 1 else stages[bit - 2, i]
                    got = jnp.where(near, before, stages[bit - 1, i])
                    if final:
                        a_parts[s][side * HALF + i - s * HALF] = got
                    else:
                        stages[bit - 1, i] = got
                if final:
                    last(s, j - s * A_STEPS).start()

        if not final:
            stage(bit + 1, j).start()

    lag = 4

    def pass_all(i):
        for bit in range(1, bits):
            j2 = i - lag * bit

            @pl.when((j2 >= 0) & (j2 < 2 * SECTIONS * A_STEPS) & (lax.rem(j2, 2) == 0))
            def _():
                pass_a(bit, lax.div(j2, 2))

    def step(i):
        hop(i)
        pass_all(i)

    start = STEPS + SKEW * (n_row - 1)

    first = 4

    @pl.loop(0, first)
    def _(i):
        step(i)

    for k in range(1, n_col):
        along_col(k).wait_recv()

    for s in range(SECTIONS):
        staged[s, 0] = every[tags[s], my_row, 0]
        staged[s, 1] = every[my_col, owners[s], 1 + lax.rem(tags[s], ratio)]
    tables = pltpu.make_async_copy(staged, table, local)
    tables.start()

    sides = []
    for s in range(SECTIONS):
        rows = [every[tags[s], r, 0].astype(jnp.float32).T[0:tile_rows] for r in range(n_row)]
        sides.append(jnp.concatenate(rows, axis=0))
    blocks = lax.broadcasted_iota(jnp.int32, (n_row * tile_rows, TILE), 0) // tile_rows * n_col
    me = my_row * n_col + my_col
    lower = jnp.zeros((n_row * tile_rows, TILE), jnp.float32)
    chosen = jnp.zeros((n_row * tile_rows, TILE), jnp.float32)
    for c in range(n_col):
        common = jnp.zeros((n_row * tile_rows, TILE), jnp.float32)
        for s in range(SECTIONS):
            tile_flags = every[c, owners[s], 1 + lax.rem(tags[s], ratio)].astype(jnp.float32)
            common += jnp.dot(sides[s], tile_flags, preferred_element_type=jnp.float32)
        occupied = jnp.where(common > 0.5, 1.0, 0.0)
        lower += jnp.where(blocks + c < me, occupied, 0.0)
        chosen += jnp.where(my_col == c, occupied, 0.0)
    occ[...] = chosen
    offset = jnp.sum(jnp.sum(lower, axis=1, keepdims=True), axis=0, keepdims=True)
    meta[0:tile_rows] = occ[pl.ds(pl.multiple_of(my_row * tile_rows, tile_rows), tile_rows)].astype(jnp.int32)
    meta[tile_rows:] = jnp.broadcast_to(offset, (8, TILE)).astype(jnp.int32)
    tables.wait()

    @pl.loop(first, start)
    def _(i):
        step(i)

    def put(ref, p, cols, rank, flag_at, part, base):
        for q in range(cols):
            here = flag_at(q)
            spot = tile_at(ref, p, q)
            got = part[base + jnp.minimum(rank, MOST - 1)]
            spot[...] = jnp.where(here == 1, got, jnp.zeros_like(got))
            rank = rank + here
        return rank

    def spread_a(s, p, rank):
        return put(a_full, p, panel, rank, lambda q: table[s, 0, q, p], a_parts[s], 0)

    def spread_b(s, p, rank):
        base = jnp.where((owners[s] >= my_row) & (my_row < n_row - 1), MOST, 0)
        return put(b_full, p, tile_cols, rank, lambda q: table[s, 1, p, q], b_parts[s], base)

    for j in range(A_STEPS):
        last(0, j).wait_recv()

    def fill_first(c, ranks):
        rank_a, rank_b = ranks
        step(start + c)
        for k in range(tile_rows // panel):
            rank_a = spread_a(0, c * (tile_rows // panel) + k, rank_a)
        rank_b = spread_b(0, c, rank_b)
        return rank_a, rank_b

    lax.fori_loop(0, panel, fill_first, (jnp.int32(0), jnp.int32(0)))

    across = tile_cols * TILE // BLOCK
    down_blocks = tile_rows * TILE // BLOCK
    pieces = across * down_blocks

    for h, acc in enumerate((acc0, acc1)):

        @pl.loop(0, pieces // 2)
        def _(j):
            step(start + panel + h * (pieces // 2) + j)
            i = lax.div(j, across)
            rows, cols = block_at(h * (down_blocks // 2) + i), block_at(lax.rem(j, across))
            acc[block_at(i), cols] = jnp.dot(a_full[rows, :], b_full[:, cols], preferred_element_type=jnp.float32)

    @pl.loop(panel + pieces, STEPS - panel)
    def _(c):
        step(start + c)

    for j in range(A_STEPS):
        last(1, j).wait_recv()

    def fill_second(c, rank_a):
        step(start + STEPS - panel + c)
        for k in range(tile_rows // panel):
            rank_a = spread_a(1, c * (tile_rows // panel) + k, rank_a)
        return rank_a

    lax.fori_loop(0, panel, fill_second, jnp.int32(0))
    lax.fori_loop(0, panel, functools.partial(spread_b, 1), jnp.int32(0))

    for k in range(1, n_row):
        along_row(k).wait_send()
    for k in range(1, n_col):
        along_col(k).wait_send()
    core_swap().wait_send()
    for s in range(SECTIONS):

        @pl.loop(0, A_STEPS)
        def _(j):
            last(s, j).wait_send()

        @pl.loop(0, STEPS)
        def _(c):
            @pl.when((my_row > 0) & (my_row < n_row - 1))
            def _():
                up(s, c).wait_send()
                down(s, c).wait_send()

    for bit in range(1, bits):

        @pl.loop(0, SECTIONS * A_STEPS)
        def _(j):
            stage(bit, j).wait_send()


def final_kernel(tile_rows, tile_cols, meta_in, acc0, acc1, a_full, b_full, out, places, meta, done, zero, local, sem):
    load = pltpu.make_async_copy(meta_in, meta, local)
    load.start()
    zero[...] = jnp.zeros_like(zero)
    across = tile_cols * TILE // BLOCK
    down = tile_rows * TILE // BLOCK
    span = BLOCK // TILE
    load.wait()

    def slab(h, acc, i, rank):
        rows = block_at(h * (down // 2) + i)

        @pl.loop(0, across)
        def _(j):
            cols = block_at(j)
            got = jnp.dot(a_full[rows, :], b_full[:, cols], preferred_element_type=jnp.float32)
            done[rows, cols] = (acc[block_at(i), cols] + got).astype(done.dtype)

        def lap(r, rank):
            p = (h * (down // 2) + i) * span + r
            for q in range(tile_cols):
                here = meta[p, q]

                @pl.when(here == 1)
                def _():
                    spot = tile_at(out, lax.div(rank, tile_cols), lax.rem(rank, tile_cols))
                    pltpu.make_async_copy(tile_at(done, p, q), spot, sem).start()

                rank = rank + here
            return rank

        return lax.fori_loop(0, span, lap, rank)

    filled = jnp.int32(0)
    for h, acc in enumerate((acc0, acc1)):
        filled = lax.fori_loop(0, down // 2, functools.partial(slab, h, acc), filled)

    @pl.loop(filled, tile_rows * tile_cols)
    def _(k):
        pltpu.make_async_copy(zero, tile_at(out, lax.div(k, tile_cols), lax.rem(k, tile_cols)), sem).start()

    down_slots = lax.broadcasted_iota(jnp.int32, places.shape, 0) * tile_cols
    slot = down_slots + lax.broadcasted_iota(jnp.int32, places.shape, 1)
    places[...] = jnp.where(slot < filled, meta[tile_rows, 0] + slot, -1)
    pltpu.make_async_copy(done, out, sem).wait()


def in_hbm(x):
    return pltpu.with_memory_space_constraint(x, pltpu.HBM)


def in_vmem(x):
    return pltpu.with_memory_space_constraint(x, pltpu.VMEM)


def shards(n_row, n_col, a_matrix, a_flags, b_matrix, b_flags, sections):
    tile_rows, panel = a_flags.shape
    tile_cols = b_flags.shape[1]
    ratio = n_col // n_row
    dtype = a_matrix.dtype
    bits = n_col.bit_length() - 1
    dma = pltpu.SemaphoreType.DMA

    def tiles(*lead):
        return lead + (TILE, TILE)

    own_a, own_b, flags = pl.pallas_call(
        functools.partial(pack_kernel, tile_rows, panel, tile_cols, ratio),
        out_shape=(
            pltpu.VMEM(tiles(MOST), dtype),
            pltpu.VMEM(tiles(SECTIONS, MOST), dtype),
            pltpu.VMEM((1 + ratio, panel, TILE), jnp.int32),
        ),
        in_specs=[HBM] * 5,
        out_specs=(VMEM, VMEM, VMEM),
        scratch_shapes=[
            pltpu.SMEM((SECTIONS,), jnp.int32),
            pltpu.SMEM((panel, tile_rows), jnp.int32),
            pltpu.SMEM(b_flags.shape, jnp.int32),
            pltpu.VMEM((panel, tile_rows), jnp.int32),
            pltpu.VMEM(b_flags.shape, jnp.int32),
            dma((5,)), dma,
        ],
        compiler_params=pltpu.CompilerParams(vmem_limit_bytes=16 * 1024 * 1024),
        name="pack",
    )(*[in_hbm(x) for x in (sections, a_flags.T, b_flags, a_matrix, b_matrix)])

    size = (tile_rows * TILE, tile_cols * TILE)
    acc0, acc1, a_full, b_full, meta = pl.pallas_call(
        functools.partial(comm_kernel, n_row, n_col, tile_rows, panel, tile_cols, ratio),
        out_shape=(
            pltpu.VMEM((size[0] // 2, size[1]), jnp.float32),
            pltpu.VMEM((size[0] // 2, size[1]), jnp.float32),
            pltpu.VMEM((tile_rows * TILE, panel * TILE), dtype),
            pltpu.VMEM((panel * TILE, tile_cols * TILE), dtype),
            pltpu.VMEM((tile_rows + 8, TILE), jnp.int32),
        ),
        in_specs=[HBM, VMEM, VMEM, VMEM],
        out_specs=(VMEM,) * 5,
        scratch_shapes=[
            pltpu.SMEM((SECTIONS,), jnp.int32),
            pltpu.VMEM((n_col, n_row, 1 + ratio, panel, TILE), jnp.int32),
            pltpu.VMEM((SECTIONS, 2, panel, TILE), jnp.int32),
            pltpu.SMEM((SECTIONS, 2, panel, TILE), jnp.int32),
            pltpu.VMEM((n_row * tile_rows, TILE), jnp.float32),
            pltpu.VMEM(tiles(HALF), dtype),
            pltpu.VMEM(tiles(MOST), dtype),
            pltpu.VMEM(tiles(MOST), dtype),
            pltpu.VMEM(tiles(MOST), dtype),
            pltpu.VMEM(tiles(2 * MOST), dtype),
            pltpu.VMEM(tiles(2 * MOST), dtype),
            pltpu.VMEM(tiles(bits - 1, MOST), dtype),
            dma, dma, dma((n_row,)), dma((n_row,)), dma((n_col,)), dma((n_col,)),
            dma((SECTIONS * STEPS,)), dma((SECTIONS * STEPS,)), dma((SECTIONS * STEPS,)), dma((SECTIONS * STEPS,)),
            dma, dma,
            dma((bits - 1, SECTIONS * A_STEPS)), dma((bits - 1, SECTIONS * A_STEPS)),
            dma((SECTIONS * A_STEPS,)), dma((SECTIONS * A_STEPS,)),
        ],
        compiler_params=pltpu.CompilerParams(
            collective_id=0, has_side_effects=True, vmem_limit_bytes=24 * 1024 * 1024
        ),
        name="exchange",
    )(in_hbm(sections), *[in_vmem(x) for x in (own_a, own_b, flags)])

    return pl.pallas_call(
        functools.partial(final_kernel, tile_rows, tile_cols),
        out_shape=(jax.ShapeDtypeStruct(size, dtype), jax.ShapeDtypeStruct((tile_rows, tile_cols), jnp.int32)),
        in_specs=[VMEM] * 5,
        out_specs=(HBM, VMEM),
        scratch_shapes=[
            pltpu.SMEM(meta.shape, jnp.int32), pltpu.VMEM(size, dtype), pltpu.VMEM((TILE, TILE), dtype), dma, dma
        ],
        compiler_params=pltpu.CompilerParams(vmem_limit_bytes=12 * 1024 * 1024),
        name="compact",
    )(*[in_vmem(x) for x in (meta, acc0, acc1, a_full, b_full)])


def solution(mesh):
    return jax.shard_map(
        functools.partial(shards, mesh.shape["row"], mesh.shape["col"]),
        mesh=mesh,
        in_specs=(P("row", "col"), P("row", "col"), P("row", "col"), P("row", "col"), P()),
        out_specs=(P("row", "col"), P("row", "col")),
        check_vma=False,
    )
```

time: 512 us -> 136 us (0.27)
  Pallas kernels: 494 us -> 134 us
  local copies, waits for them, and re-layouts: 15.7 us -> 0 us
    pallas_call x1, Pallas kernels: 486 us -> 118 us  [shards(): pl.pallas_call(functools.partial(comm_kernel, n_row, n_col, tile_rows, pa...]
    unnamed x19 -> x0, local copies, waits for them, and re-layouts: 15.7 us -> none
    pallas_call x1, Pallas kernels: 4.51 us -> 15.7 us  [shards(): pl.pallas_call(functools.partial(final_kernel, tile_rows, tile_cols), out...]
where the time goes in v2:
time: 136 us; the launch traced here: 135 us
  Pallas kernels  134 us (99%)
    pallas_call x1, Pallas kernels, shards(): pl.pallas_call(functools.partial(comm_kernel, n_row, n_col, tile_rows, pa...  118 us
    pallas_call x1, Pallas kernels, shards(): pl.pallas_call(functools.partial(final_kernel, tile_rows, tile_cols), out...  15.7 us

profile of v2, /device:TPU:0, one launch (start us, length us, event | category | flops | bytes accessed | tf_op | source)
XLA Modules:
  0.0 135.1 jit_solution(15744580444163507381)
XLA Ops:
  0.6 1.0 pack.1
  1.6 117.8 %exchange.1 = (f32[1024,2048]{1,0:T(8,128)S(1)}, f32[1024,2048]{1,0:T(8,128)S(1)}, bf16[2048,1024]{1,0:T(8,128)(2,1)S(1)}, bf16[1024,2048]{1,0:T(8,128)(2,1)S(1)}, s32[24,128]{1,0:T(8,128)S(1)}) custom-call(s32[2]{0:T(128)} %sections_in.3, bf16[64,128,128]{2,1,0:T(8,128)(2,1)S(1)} %get-tuple-element.10.own_a, ...), custom_call_target="tpu_custom_call" | custom-call | tf_op jit(solution)/shard_map/exchange/pallas_call | solution.py:488
  119.4 15.7 %compact.1 = (bf16[2048,2048]{1,0:T(8,128)(2,1)}, s32[16,16]{1,0:T(8,128)}) custom-call(s32[24,128]{1,0:T(8,128)S(1)} %get-tuple-element.13.meta_in, f32[1024,2048]{1,0:T(8,128)S(1)} %get-tuple-element.14.acc0, f32[1024,2048]{1,0:T(8,128)S(1)} %get-tuple-element.15.acc1, bf16[2048,1024]{1,0:T(8,128)(2,1)S(1)} %get-tuple-element.16.a_full, ...), custom_call_target="tpu_custom_call" | custom-call | tf_op jit(solution)/shard_map/compact/pallas_call | solution.py:524

commit v3 on v1

v3 whole, which is shorter than its diff:
```python
import functools

import jax
import jax.numpy as jnp
from jax import lax
from jax.experimental import pallas as pl
from jax.experimental.pallas import tpu as pltpu
from jax.sharding import PartitionSpec as P

TILE = 128
SECTIONS = 2
MOST = 64
HALF = MOST // 2
SPAN = 2
LOW = MOST // SPAN
LENGTHS = (64, 80, 88, 96, 104, 112, 128)
A_SPAN = 4
A_STEPS = HALF // A_SPAN
BLOCK = 512
SKEW = 3
MESH = pl.DeviceIdType.MESH
HBM = pl.BlockSpec(memory_space=pltpu.HBM)
SMEM = pl.BlockSpec(memory_space=pltpu.SMEM)
VMEM = pl.BlockSpec(memory_space=pltpu.VMEM)


def tile_at(ref, p, q):
    rows = pl.ds(pl.multiple_of(p * TILE, TILE), TILE)
    cols = pl.ds(q * TILE if isinstance(q, int) else pl.multiple_of(q * TILE, TILE), TILE)
    return ref.at[rows, cols]


def block_at(j, size=BLOCK):
    return pl.ds(pl.multiple_of(j * size, size), size)


def pack_kernel(
    tile_rows, panel, tile_cols, ratio, sections_in, a_flags_in, b_flags_in, a, b,
    a_out, b_out, flags, sections, a_flags, b_flags, a_vec, b_vec, sems, sem,
):
    moves = (
        (sections_in, sections), (b_flags_in, b_flags), (a_flags_in, a_flags), (a_flags_in, a_vec), (b_flags_in, b_vec)
    )
    loads = [pltpu.make_async_copy(src, dst, sems.at[i]) for i, (src, dst) in enumerate(moves)]
    for load in loads:
        load.start()
    flags[...] = jnp.zeros_like(flags)
    for load in loads:
        load.wait()

    def gather(occupied, src, out, base, rows, cols, first, turned):
        def lap(p, rank):
            for q in range(cols):
                here = occupied[q, p] if turned else occupied[first + p, q]

                @pl.when(here == 1)
                def _():
                    pltpu.make_async_copy(tile_at(src, first + p, q), out.at[base + rank], sem).start()

                rank = rank + here
            return rank

        return lax.fori_loop(0, rows, lap, jnp.int32(0))

    total = jnp.int32(0)
    my_row, my_col = lax.axis_index("row"), lax.axis_index("col")
    mine_a = (sections[0] == my_col) | (sections[1] == my_col)
    for s in range(SECTIONS):
        first = lax.rem(sections[s], ratio) * panel
        total += lax.cond(
            sections[s] // ratio == my_row,
            lambda: gather(b_flags, b, b_out, s * MOST, panel, tile_cols, first, False),
            lambda: jnp.int32(0),
        )
    total += lax.cond(mine_a, lambda: gather(a_flags, a, a_out, 0, tile_rows, panel, 0, True), lambda: jnp.int32(0))

    flags[0, :, 0:tile_rows] = a_vec[...]
    for i in range(ratio):
        flags[1 + i, :, 0:tile_cols] = b_vec[i * panel : (i + 1) * panel, :]

    @pl.loop(0, total)
    def _(i):
        pltpu.make_async_copy(tile_at(a, 0, 0), a_out.at[0], sem).wait()


def count_kernel(
    n_row, n_col, ratio, sections_in, b_flags, sums, pick,
    counts, b_vec, every, sections, local, brief, row_send, row_recv, col_send, col_recv,
):
    my_row, my_col = lax.axis_index("row"), lax.axis_index("col")
    choice = pltpu.make_async_copy(sections_in, sections, brief)
    load = pltpu.make_async_copy(b_flags, b_vec, local)
    choice.start()
    load.start()
    greet(n_row, n_col, my_row, my_col)
    choice.wait()
    load.wait()
    for s in range(SECTIONS):
        found = b_vec[lax.rem(sections[s], ratio)].astype(jnp.float32)
        found = jnp.sum(jnp.sum(found, axis=1, keepdims=True), axis=0, keepdims=True)
        found = jnp.where(lax.div(sections[s], ratio) == my_row, found, jnp.zeros_like(found))
        counts[s : s + 1, :] = jnp.broadcast_to(found, (1, TILE)).astype(jnp.int32)
    along_row, along_col = gathering(
        n_row, n_col, my_row, my_col, counts, every, row_send, row_recv, col_send, col_recv
    )
    for k in range(1, n_row):
        along_row(k).start()
    own = pltpu.make_async_copy(counts, every.at[my_col, my_row], local)
    own.start()
    own.wait()
    for k in range(1, n_row):
        along_row(k).wait_recv()
    for k in range(1, n_col):
        along_col(k).start()
    for k in range(1, n_col):
        along_col(k).wait_recv()

    again = sections[0] == sections[1]
    weight = jnp.where(again, 0, 1)
    most = jnp.zeros((1, TILE), jnp.int32)
    for c in range(0, n_col, 2):
        pair = jnp.zeros((1, TILE), jnp.int32)
        for d in (c, c + 1):
            whole = sum(every[d, r] for r in range(n_row))
            sums[d] = whole
            pair += whole[0:1] + whole[1:2] * weight
        most = jnp.maximum(most, pair)
    level = 1 + sum(jnp.where(most > 2 * length, 1, 0) for length in LENGTHS[1:-1])
    pick[...] = jnp.where(again, 0, level)

    for k in range(1, n_row):
        along_row(k).wait_send()
    for k in range(1, n_col):
        along_col(k).wait_send()


def greet(n_row, n_col, my_row, my_col):
    barrier = pltpu.get_barrier_semaphore()
    for k in range(1, n_row):
        pl.semaphore_signal(barrier, inc=1, device_id=(lax.rem(my_row + k, n_row), my_col), device_id_type=MESH)
    for k in range(1, n_col):
        pl.semaphore_signal(barrier, inc=1, device_id=(my_row, lax.rem(my_col + k, n_col)), device_id_type=MESH)
    pl.semaphore_wait(barrier, n_row + n_col - 2)


def gathering(n_row, n_col, my_row, my_col, mine, every, row_send, row_recv, col_send, col_recv):
    def along_row(k):
        return send(
            mine, every.at[my_col, my_row], row_send.at[k], row_recv.at[k], lax.rem(my_row + k, n_row), my_col
        )

    def along_col(k):
        return send(
            every.at[my_col], every.at[my_col], col_send.at[k], col_recv.at[k], my_row, lax.rem(my_col + k, n_col)
        )

    return along_row, along_col


def send(src, dst, send_sem, recv_sem, row, col):
    return pltpu.make_async_remote_copy(
        src_ref=src, dst_ref=dst, send_sem=send_sem, recv_sem=recv_sem, device_id=(row, col), device_id_type=MESH
    )


def comm_kernel(
    length, n_row, n_col, tile_rows, panel, tile_cols, ratio,
    sections_in, own_a, own_b, flags, sums, done, meta,
    sections, totals, every, staged, table, begin, occ, swapped, held, a0, a1, b_low, b_high, pal, give, got_back, stages,
    acc, a_full, b_full,
    local, brief, tiny, pal_send, pal_recv, row_send, row_recv, col_send, col_recv,
    up_send, up_recv, down_send, down_recv, give_send, give_recv,
    core_send, core_recv, stage_send, stage_recv, last_send, last_recv,
):
    my_row, my_col = lax.axis_index("row"), lax.axis_index("col")
    bits = n_col.bit_length() - 1
    side = lax.rem(my_col, 2)
    partner = my_col + 1 - 2 * side
    above = jnp.minimum(my_row + 1, n_row - 1)
    below = jnp.maximum(my_row - 1, 0)
    a_parts = (a0, a1)
    chunks = length // SPAN
    parts = [(b_low, MOST, 0, LOW)]
    if chunks > LOW:
        parts.append((b_high, length - MOST, LOW, chunks))
    once = length == MOST
    shared = length if once else 2 * length - 2 * MOST
    first_shared = shared // SPAN
    delay = SKEW * (n_row - 1)

    def flip(bit):
        on = lax.rem(lax.div(my_col, 1 << bit), 2)
        return my_col + (1 << bit) - 2 * on * (1 << bit)

    choice = pltpu.make_async_copy(sections_in, sections, brief)
    number = pltpu.make_async_copy(sums, totals, tiny)
    choice.start()
    number.start()
    greet(n_row, n_col, my_row, my_col)
    along_row, along_col = gathering(
        n_row, n_col, my_row, my_col, flags, every, row_send, row_recv, col_send, col_recv
    )
    own = pltpu.make_async_copy(flags, every.at[my_col, my_row], local)
    choice.wait()
    number.wait()
    tags = [sections[s] for s in range(SECTIONS)]
    owners = [lax.div(tag, ratio) for tag in tags]

    def up(ref, size, g, c):
        part = pl.ds(c * SPAN, SPAN)
        return send(ref.at[part], ref.at[part], up_send.at[g], up_recv.at[g], above, my_col)

    def down(ref, size, g, c):
        part = pl.ds(size + c * SPAN, SPAN)
        return send(ref.at[part], ref.at[part], down_send.at[g], down_recv.at[g], below, my_col)

    def core_swap():
        return send(own_a.at[pl.ds((1 - side) * HALF, HALF)], swapped, core_send, core_recv, my_row, partner)

    def pal_swap():
        return send(own_b.at[pl.ds(MOST, MOST)], pal, pal_send, pal_recv, my_row, partner)

    def hand(c):
        part = pl.ds(c * SPAN, SPAN)
        return send(give.at[part], got_back.at[part], give_send.at[c], give_recv.at[c], my_row, partner)

    def stage(bit, j):
        src = held if bit == 1 else stages.at[bit - 2]
        part = pl.ds(j * A_SPAN, A_SPAN)
        return send(
            src.at[part], stages.at[bit - 1, part], stage_send.at[bit - 1, j], stage_recv.at[bit - 1, j],
            my_row, flip(bit),
        )

    def last(s, j):
        part = pl.ds(side * HALF + j * A_SPAN, A_SPAN)
        i = s * A_STEPS + j
        return send(a_parts[s].at[part], a_parts[s].at[part], last_send.at[i], last_recv.at[i], my_row, partner)

    core_swap().start()
    if not once:
        pal_swap().start()
    own.start()
    for k in range(1, n_row):
        along_row(k).start()

    again = tags[0] == tags[1]
    count = totals[my_col, 0, 0]
    pal_count = totals[partner, 0, 0]
    filled = count + jnp.where(again, 0, totals[my_col, 1, 0])
    shift = jnp.where(again, 0, count)

    def listed(slot, with_pal):
        at = jnp.where(slot < count, slot, MOST + jnp.clip(slot - count, 0, MOST - 1))
        if not with_pal:
            return own_b[at]
        from_pal = jnp.clip(2 * length - 1 - slot - pal_count, 0, MOST - 1)
        return jnp.where(slot < filled, own_b[at], pal[from_pal])

    def parted(g, body):
        for ref, size, begins, ends in parts:

            @pl.when((g >= begins) & (g < ends))
            def _():
                body(ref, size, g, g - begins)

    def feed(way, region, with_pal, ref, size, g, c):
        for k in range(SPAN):
            ref[region * size + c * SPAN + k] = listed(g * SPAN + k, with_pal)
        way(ref, size, g, c).start()

    def take(way, region, onward, with_pal, ref, size, g, c):
        way(ref, size, g, c).wait_recv()
        for k in range(SPAN):
            slot = g * SPAN + k
            spot = region * size + c * SPAN + k
            mine = jnp.where(slot < count, owners[0], owners[1]) == my_row
            ref[spot] = jnp.where(mine, listed(slot, with_pal), ref[spot])

        @pl.when(onward)
        def _():
            way(ref, size, g, c).start()

    def lower_of(s):
        return (owners[s] >= my_row) & (my_row < n_row - 1)

    def hand_over(ref, size, g, c):
        for k in range(SPAN):
            here = c * SPAN + k
            got = jnp.where(lower_of(1), ref[size + here], ref[here])
            give[g * SPAN + k - shared] = got
        hand(g - first_shared).start()

    def hop(i, with_pal):
        @pl.when(my_row == 0)
        def _():
            parted(i, functools.partial(feed, up, 0, with_pal))

        @pl.when(my_row == n_row - 1)
        def _():
            parted(i, functools.partial(feed, down, 1, with_pal))

        @pl.when(my_row > 0)
        def _():
            parted(i - SKEW * my_row, functools.partial(take, up, 0, my_row < n_row - 1, with_pal))

        @pl.when(my_row < n_row - 1)
        def _():
            parted(i - SKEW * (n_row - 1 - my_row), functools.partial(take, down, 1, my_row > 0, with_pal))

        if with_pal and first_shared < chunks:

            @pl.when(i - delay >= first_shared)
            def _():
                parted(i - delay, hand_over)

    def pass_a(bit, j):
        stage(bit, j).wait_recv()
        final = bit == bits - 1
        for s in range(SECTIONS):

            @pl.when((j >= s * A_STEPS) & (j < (s + 1) * A_STEPS))
            def _():
                near = lax.div(tags[s], 1 << bit) == lax.div(my_col, 1 << bit)
                for k in range(A_SPAN):
                    i = j * A_SPAN + k
                    before = held[i] if bit == 1 else stages[bit - 2, i]
                    got = jnp.where(near, before, stages[bit - 1, i])
                    if final:
                        a_parts[s][side * HALF + i - s * HALF] = got
                    else:
                        stages[bit - 1, i] = got
                if final:
                    last(s, j - s * A_STEPS).start()

        if not final:
            stage(bit + 1, j).start()

    lag = 4

    def pass_all(i):
        for bit in range(1, bits):
            j2 = i - lag * bit

            @pl.when((j2 >= 0) & (j2 < 2 * SECTIONS * A_STEPS) & (lax.rem(j2, 2) == 0))
            def _():
                pass_a(bit, lax.div(j2, 2))

    def step(i, with_pal=True):
        hop(i, with_pal)
        pass_all(i)

    def send_a():
        core_swap().wait_recv()
        for s in range(SECTIONS):
            mine = tags[s] == my_col

            @pl.loop(0, HALF)
            def _(k):
                held[s * HALF + k] = jnp.where(mine, own_a[side * HALF + k], swapped[k])

        @pl.loop(0, SECTIONS * A_STEPS)
        def _(j):
            stage(1, j).start()

    start = LOW + delay
    early = min(first_shared, start - 16)
    opening = 2

    def survey():
        for k in range(1, n_col):
            along_col(k).wait_recv()
        for s in range(SECTIONS):
            staged[s, 0] = every[tags[s], my_row, 0]
            staged[s, 1] = every[my_col, owners[s], 1 + lax.rem(tags[s], ratio)]
        tables = pltpu.make_async_copy(staged, table, local)
        tables.start()
        sides = []
        for s in range(SECTIONS):
            rows = [every[tags[s], r, 0].astype(jnp.float32).T[0:tile_rows] for r in range(n_row)]
            sides.append(jnp.concatenate(rows, axis=0))
        blocks = lax.broadcasted_iota(jnp.int32, (n_row * tile_rows, TILE), 0) // tile_rows * n_col
        me = my_row * n_col + my_col
        lower = jnp.zeros((n_row * tile_rows, TILE), jnp.float32)
        chosen = jnp.zeros((n_row * tile_rows, TILE), jnp.float32)
        for c in range(n_col):
            common = jnp.zeros((n_row * tile_rows, TILE), jnp.float32)
            for s in range(SECTIONS):
                tile_flags = every[c, owners[s], 1 + lax.rem(tags[s], ratio)].astype(jnp.float32)
                common += jnp.dot(sides[s], tile_flags, preferred_element_type=jnp.float32)
            occupied = jnp.where(common > 0.5, 1.0, 0.0)
            lower += jnp.where(blocks + c < me, occupied, 0.0)
            chosen += jnp.where(my_col == c, occupied, 0.0)
        occ[...] = chosen
        offset = jnp.sum(jnp.sum(lower, axis=1, keepdims=True), axis=0, keepdims=True)
        mine = pl.ds(pl.multiple_of(my_row * tile_rows, tile_rows), tile_rows)
        meta[0:tile_rows] = occ[mine].astype(jnp.int32)
        meta[tile_rows:] = jnp.broadcast_to(offset, (8, TILE)).astype(jnp.int32)

        tables.wait()
        for s in range(SECTIONS):

            def lap_a(p, rank):
                begin[s, 0, p] = rank
                for q in range(panel):
                    rank = rank + table[s, 0, q, p]
                return rank

            def lap_b(p, rank):
                begin[s, 1, p] = rank
                for q in range(tile_cols):
                    rank = rank + table[s, 1, p, q]
                return rank

            lax.fori_loop(0, tile_rows, lap_a, jnp.int32(0))
            lax.fori_loop(0, panel, lap_b, jnp.int32(0))

    def relay():
        own.wait()
        for k in range(1, n_row):
            along_row(k).wait_recv()
        for k in range(1, n_col):
            along_col(k).start()

    @pl.loop(0, early)
    def _(i):
        step(i, False)

        @pl.when(i == opening)
        def _():
            relay()
            send_a()

    if not once:
        pal_swap().wait_recv()

    def put(ref, p, cols, rank, flag_at, load):
        for q in range(cols):
            here = flag_at(q)
            got = load(rank)
            tile_at(ref, p, q)[...] = jnp.where(here == 1, got, jnp.zeros_like(got))
            rank = rank + here

    double = tile_rows // panel

    def spread_a(s, u):
        for k in range(double):
            p = u * double + k
            put(
                a_full, p, panel, begin[s, 0, p], lambda q: table[s, 0, q, p],
                lambda rank: a_parts[s][jnp.minimum(rank, MOST - 1)],
            )

    def spread_b0(p):
        base = jnp.where(lower_of(0), MOST, 0)
        put(
            b_full, p, tile_cols, begin[0, 1, p], lambda q: table[0, 1, p, q],
            lambda rank: b_low[base + jnp.minimum(rank, MOST - 1)],
        )

    def spread_b1(p):
        low = lower_of(1)

        def load(rank):
            place = shift + rank
            got = b_low[jnp.where(low, MOST, 0) + jnp.minimum(place, MOST - 1)]
            if length > MOST:
                size = length - MOST
                at = jnp.where(low, size, 0) + jnp.clip(place - MOST, 0, size - 1)
                got = jnp.where(place < MOST, got, b_high[at])
            if shared < length:
                got = jnp.where(place < length, got, got_back[jnp.clip(2 * MOST - 1 - place, 0, length - shared - 1)])
            return got

        put(b_full, p, tile_cols, begin[1, 1, p], lambda q: table[1, 1, p, q], load)

    across = tile_cols * TILE // BLOCK
    pieces = across * (tile_rows * TILE // BLOCK)

    def multiply(j):
        rows, cols = block_at(lax.div(j, across)), block_at(lax.rem(j, across))
        return rows, cols, jnp.dot(a_full[rows, :], b_full[:, cols], preferred_element_type=jnp.float32)

    def multiply_first(j):
        rows, cols, got = multiply(j)
        acc[rows, cols] = got

    def a_here(s):
        for j in range(A_STEPS):
            last(s, j).wait_recv()

    spare = chunks - LOW
    light = spare // 8
    plan = [(start - panel, panel, panel, lambda: a_here(0), functools.partial(spread_a, 0))]
    if once:
        plan.append((start, 0, panel, None, spread_b0))
    else:
        plan.append((start, light, panel, None, spread_b0))
        plan.append((start + light, spare - 2 * light, pieces, None, multiply_first))
        plan.append((start + spare - light, light, panel, lambda: a_here(1), functools.partial(spread_a, 1)))

    @pl.loop(early, chunks + delay)
    def _(i):
        step(i)

        @pl.when(i == early + 1)
        def _():
            survey()

        for begins, steps, units, before, body in plan:
            if steps:
                per = -(-units // steps)
                c = i - begins

                @pl.when((c >= 0) & (c < steps))
                def _():
                    if before is not None:

                        @pl.when(c == 0)
                        def _():
                            before()

                    @pl.loop(c * per, jnp.minimum((c + 1) * per, units))
                    def _(u):
                        body(u)

    for begins, steps, units, before, body in plan:
        if not steps:
            if before is not None:
                before()

            @pl.loop(0, units)
            def _(u):
                body(u)

    if first_shared < chunks:

        @pl.loop(0, chunks - first_shared)
        def _(c):
            hand(c).wait_recv()

    if once:
        a_here(1)
    else:

        @pl.loop(0, panel)
        def _(p):
            spread_b1(p)

    @pl.loop(0, pieces)
    def _(j):
        rows, cols, got = multiply(j)
        done[rows, cols] = (got + got if once else acc[rows, cols] + got).astype(done.dtype)

    for k in range(1, n_row):
        along_row(k).wait_send()
    for k in range(1, n_col):
        along_col(k).wait_send()
    if not once:
        pal_swap().wait_send()
    core_swap().wait_send()
    if first_shared < chunks:

        @pl.loop(0, chunks - first_shared)
        def _(c):
            hand(c).wait_send()

    for s in range(SECTIONS):

        @pl.loop(0, A_STEPS)
        def _(j):
            last(s, j).wait_send()

    for ref, size, begins, ends in parts:

        @pl.loop(begins, ends)
        def _(g):
            @pl.when(my_row < n_row - 1)
            def _():
                up(ref, size, g, g - begins).wait_send()

            @pl.when(my_row > 0)
            def _():
                down(ref, size, g, g - begins).wait_send()

    for bit in range(1, bits):

        @pl.loop(0, SECTIONS * A_STEPS)
        def _(j):
            stage(bit, j).wait_send()


def final_kernel(tile_rows, tile_cols, meta_in, done, out, places, meta, zero, local, sem):
    load = pltpu.make_async_copy(meta_in, meta, local)
    load.start()
    zero[...] = jnp.zeros_like(zero)
    load.wait()

    def lap(p, rank):
        for q in range(tile_cols):
            here = meta[p, q]

            @pl.when(here == 1)
            def _():
                spot = tile_at(out, lax.div(rank, tile_cols), lax.rem(rank, tile_cols))
                pltpu.make_async_copy(tile_at(done, p, q), spot, sem).start()

            rank = rank + here
        return rank

    filled = lax.fori_loop(0, tile_rows, lap, jnp.int32(0))

    @pl.loop(filled, tile_rows * tile_cols)
    def _(k):
        pltpu.make_async_copy(zero, tile_at(out, lax.div(k, tile_cols), lax.rem(k, tile_cols)), sem).start()

    down_slots = lax.broadcasted_iota(jnp.int32, places.shape, 0) * tile_cols
    slot = down_slots + lax.broadcasted_iota(jnp.int32, places.shape, 1)
    places[...] = jnp.where(slot < filled, meta[tile_rows, 0] + slot, -1)
    pltpu.make_async_copy(done, out, sem).wait()


def in_hbm(x):
    return pltpu.with_memory_space_constraint(x, pltpu.HBM)


def in_vmem(x):
    return pltpu.with_memory_space_constraint(x, pltpu.VMEM)


def shards(n_row, n_col, a_matrix, a_flags, b_matrix, b_flags, sections):
    tile_rows, panel = a_flags.shape
    tile_cols = b_flags.shape[1]
    ratio = n_col // n_row
    dtype = a_matrix.dtype
    bits = n_col.bit_length() - 1
    dma = pltpu.SemaphoreType.DMA

    def tiles(*lead):
        return lead + (TILE, TILE)

    size = (tile_rows * TILE, tile_cols * TILE)
    sums, pick = pl.pallas_call(
        functools.partial(count_kernel, n_row, n_col, ratio),
        out_shape=(
            jax.ShapeDtypeStruct((n_col, SECTIONS, TILE), jnp.int32), jax.ShapeDtypeStruct((1, TILE), jnp.int32)
        ),
        in_specs=[HBM, HBM],
        out_specs=(VMEM, VMEM),
        scratch_shapes=[
            pltpu.VMEM((SECTIONS, TILE), jnp.int32),
            pltpu.VMEM((ratio, panel, tile_cols), jnp.int32),
            pltpu.VMEM((n_col, n_row, SECTIONS, TILE), jnp.int32),
            pltpu.SMEM((SECTIONS,), jnp.int32), dma, dma, dma((n_row,)), dma((n_row,)), dma((n_col,)), dma((n_col,))
        ],
        compiler_params=pltpu.CompilerParams(
            collective_id=len(LENGTHS), has_side_effects=True, vmem_limit_bytes=8 * 1024 * 1024
        ),
        name="counts",
    )(in_hbm(sections), in_hbm(b_flags.reshape(ratio, panel, tile_cols)))

    def exchange(level, sections, a_flags, b_flags, a, b, sums):
        own_a, own_b, flags = pl.pallas_call(
            functools.partial(pack_kernel, tile_rows, panel, tile_cols, ratio),
            out_shape=(
                pltpu.VMEM(tiles(MOST), dtype),
                pltpu.VMEM(tiles(SECTIONS * MOST), dtype),
                pltpu.VMEM((1 + ratio, panel, TILE), jnp.int32),
            ),
            in_specs=[HBM] * 5,
            out_specs=(VMEM,) * 3,
            scratch_shapes=[
                pltpu.SMEM((SECTIONS,), jnp.int32),
                pltpu.SMEM((panel, tile_rows), jnp.int32),
                pltpu.SMEM(b_flags.shape, jnp.int32),
                pltpu.VMEM((panel, tile_rows), jnp.int32),
                pltpu.VMEM(b_flags.shape, jnp.int32),
                dma((5,)), dma,
            ],
            compiler_params=pltpu.CompilerParams(vmem_limit_bytes=16 * 1024 * 1024),
            name="pack",
        )(*[in_hbm(x) for x in (sections, a_flags, b_flags, a, b)])

        length = LENGTHS[level]
        chunks = length // SPAN
        handed = SPAN if level == 0 else max(2 * MOST - length, SPAN)
        done, meta = pl.pallas_call(
            functools.partial(comm_kernel, length, n_row, n_col, tile_rows, panel, tile_cols, ratio),
            out_shape=(
                pltpu.VMEM(size, dtype),
                pltpu.VMEM((tile_rows + 8, TILE), jnp.int32),
            ),
            in_specs=[HBM, VMEM, VMEM, VMEM, HBM],
            out_specs=(VMEM,) * 2,
            scratch_shapes=[
                pltpu.SMEM((SECTIONS,), jnp.int32),
                pltpu.SMEM((n_col, SECTIONS, TILE), jnp.int32),
                pltpu.VMEM((n_col, n_row, 1 + ratio, panel, TILE), jnp.int32),
                pltpu.VMEM((SECTIONS, 2, panel, TILE), jnp.int32),
                pltpu.SMEM((SECTIONS, 2, panel, TILE), jnp.int32),
                pltpu.SMEM((SECTIONS, 2, tile_rows), jnp.int32),
                pltpu.VMEM((n_row * tile_rows, TILE), jnp.float32),
                pltpu.VMEM(tiles(HALF), dtype),
                pltpu.VMEM(tiles(MOST), dtype),
                pltpu.VMEM(tiles(MOST), dtype),
                pltpu.VMEM(tiles(MOST), dtype),
                pltpu.VMEM(tiles(2 * MOST), dtype),
                pltpu.VMEM(tiles(2 * max(length - MOST, 1)), dtype),
                pltpu.VMEM(tiles(MOST), dtype),
                pltpu.VMEM(tiles(handed), dtype),
                pltpu.VMEM(tiles(handed), dtype),
                pltpu.VMEM(tiles(bits - 1, MOST), dtype),
                pltpu.VMEM(size if level else (8, TILE), jnp.float32),
                pltpu.VMEM((tile_rows * TILE, panel * TILE), dtype),
                pltpu.VMEM((panel * TILE, tile_cols * TILE), dtype),
                dma, dma, dma, dma, dma, dma((n_row,)), dma((n_row,)), dma((n_col,)), dma((n_col,)),
                dma((chunks,)), dma((chunks,)), dma((chunks,)), dma((chunks,)),
                dma((handed // SPAN,)), dma((handed // SPAN,)),
                dma, dma,
                dma((bits - 1, SECTIONS * A_STEPS)), dma((bits - 1, SECTIONS * A_STEPS)),
                dma((SECTIONS * A_STEPS,)), dma((SECTIONS * A_STEPS,)),
            ],
            compiler_params=pltpu.CompilerParams(
                collective_id=level, has_side_effects=True, vmem_limit_bytes=49 * 1024 * 1024
            ),
            name=f"exchange_{length}",
        )(in_hbm(sections), *[in_vmem(x) for x in (own_a, own_b, flags)], in_hbm(sums))

        return pl.pallas_call(
            functools.partial(final_kernel, tile_rows, tile_cols),
            out_shape=(jax.ShapeDtypeStruct(size, dtype), jax.ShapeDtypeStruct((tile_rows, tile_cols), jnp.int32)),
            in_specs=[VMEM] * 2,
            out_specs=(HBM, VMEM),
            scratch_shapes=[
                pltpu.SMEM(meta.shape, jnp.int32), pltpu.VMEM((TILE, TILE), dtype), dma, dma
            ],
            compiler_params=pltpu.CompilerParams(vmem_limit_bytes=12 * 1024 * 1024),
            name="compact",
        )(*[in_vmem(x) for x in (meta, done)])

    branches = [functools.partial(exchange, level) for level in range(len(LENGTHS))]
    return lax.switch(pick[0, 0], branches, sections, a_flags.T, b_flags, a_matrix, b_matrix, sums)


def solution(mesh):
    return jax.shard_map(
        functools.partial(shards, mesh.shape["row"], mesh.shape["col"]),
        mesh=mesh,
        in_specs=(P("row", "col"), P("row", "col"), P("row", "col"), P("row", "col"), P()),
        out_specs=(P("row", "col"), P("row", "col")),
        check_vma=False,
    )
```

time: 512 us -> 129 us (0.25)
  Pallas kernels: 494 us -> 127 us
  local copies, waits for them, and re-layouts: 15.7 us -> 0 us
    pallas_call x3 -> x4, Pallas kernels: 494 us -> 127 us  [the longest x1 109 us: exchange(): pl.pallas_call(functools.partial(comm_kernel, length, n_row, n_col, tile_...]
    unnamed x19 -> x0, local copies, waits for them, and re-layouts: 15.7 us -> none
where the time goes in v3:
time: 129 us
  Pallas kernels  127 us (98%)
    pallas_call x1, Pallas kernels, exchange(): pl.pallas_call(functools.partial(comm_kernel, length, n_row, n_col, tile_...  109 us
    pallas_call x1, Pallas kernels, shards(): pl.pallas_call(functools.partial(count_kernel, n_row, n_col, ratio), out_...  12.4 us
    pallas_call x1, Pallas kernels, exchange(): pl.pallas_call(functools.partial(final_kernel, tile_rows, tile_cols), out...  4.53 us

profile of v3, /device:TPU:0, one launch (start us, length us, event | category | flops | bytes accessed | tf_op | source)
XLA Modules:
  0.0 128.6 jit_solution(3660618485660599924)
XLA Ops:
  0.6 12.4 %counts.1 = (s32[8,2,128]{2,1,0:T(2,128)}, s32[1,128]{1,0:T(1,128)S(1)}) custom-call(s32[2]{0:T(128)} %sections_in.1, s32[2,8,16]{2,1,0:T(8,128)} %bitcast.5), custom_call_target="tpu_custom_call" | custom-call | tf_op jit(solution)/shard_map/counts/pallas_call | solution.py:643
  13.0 115.4 %conditional.1 = ((bf16[2048,2048]{1,0:T(8,128)(2,1)}, s32[16,16]{1,0:T(8,128)})) conditional(s32[]{:T(128)} %bitcast.1, (s32[2]{0:T(128)}, s32[8,16]{1,0:T(8,128)}, s32[16,16]{1,0:T(8,128)}, bf16[2048,1024]{1,0:T(8,128)(2,1)}, bf16[2048,2048]{1,0:T(8,128)(2,1)}, /*index=5*/s32[8,2,128]{2,1,0:T(2,128)}) %tuple.57, ...), branch_computations={%region_0.0_spmd, %region_1.0_spmd, %region_2.0_spmd, %region_3.0_... | conditional | bytes 8 | solution.py:742
  13.1 1.1 pack.10
  14.2 108.9 %exchange_96.1 = (bf16[2048,2048]{1,0:T(8,128)(2,1)S(1)}, s32[24,128]{1,0:T(8,128)S(1)}) custom-call(s32[2]{0:T(128)} %get-tuple-element.117.sections_in, bf16[64,128,128]{2,1,0:T(8,128)(2,1)S(1)} %get-tuple-element.122.own_a, bf16[128,128,128]{2,1,0:T(8,128)(2,1)S(1)} %get-tuple-element.123.own_b, s32[3,8,128]{2,1,0:T(8,128)S(1)} %get-tuple-element.124.flags, ...), custom_call_target="tpu_custom_call" | custom-call | tf_op jit(solution)/shard_map/cond/branch_3_fun/exchange_96/pallas_call | solution.py:687
  123.1 4.5 %compact.10 = (bf16[2048,2048]{1,0:T(8,128)(2,1)}, s32[16,16]{1,0:T(8,128)}) custom-call(s32[24,128]{1,0:T(8,128)S(1)} %get-tuple-element.126.meta_in, bf16[2048,2048]{1,0:T(8,128)(2,1)S(1)} %get-tuple-element.127.done), custom_call_target="tpu_custom_call" | custom-call | tf_op jit(solution)/shard_map/cond/branch_3_fun/compact/pallas_call | solution.py:729
